TPU v7x, 32 devices: a whole 2x2x4 slice. The times are simulated.
32 devices in a mesh: ep: 8 (over z, x), tp: 4 (over y, core).
Axes of the slice: x: 2, y: 2, z: 4, core: 2. Of those that a mesh axis runs over, the one named last changes fastest.
Arguments:
- tokens: bfloat16 [2048, 2880], P('ep', 'tp'), may hold values from -6 to 6
- expert_ids: int32 [2048, 4], P('ep'), may hold values from 0 to 15, all different within a row; in each aligned block of 256 rows (0 to 255, 256 to 511, ...) at most 128 rows name the same one
- combine_weights: float32 [2048, 4], P('ep'), may hold values from 0.05 to 0.6
- gate_weight: bfloat16 [16, 2880, 2880], P('ep', None, 'tp'), may hold values from -0.109375 to 0.109375
- up_weight: bfloat16 [16, 2880, 2880], P('ep', None, 'tp'), may hold values from -0.109375 to 0.109375
- down_weight: bfloat16 [16, 2880, 2880], P('ep', 'tp'), may hold values from -0.109375 to 0.109375
Outputs:
- mixed: bfloat16 [2048, 2880], P('ep', 'tp')
Inputs may be any that keep to these rules, and one draw needn't show every extreme that they name: `expert_ids`: each row names 4 different experts; within the 256 rows of one index of ep no expert is named more than 128 times, a bound that some block reaches.
All inputs are finite; a program needn't handle non-finite values.
Results may differ from a plain program's by a relative error of at most 0.014.
Values may be sent and summed in bfloat16 or wider, within the bound.
A program may use at most 128 MiB of HBM per device.

v0:
```python
import functools

import jax
import jax.numpy as jnp
from jax import lax
from jax.experimental import pallas as pl
from jax.experimental.pallas import tpu as pltpu
from jax.sharding import PartitionSpec as P


def activate(gate_acc, up_acc):
    return (up_acc + 1.0) * gate_acc * jax.nn.sigmoid(1.702 * gate_acc)


MESH = pl.DeviceIdType.MESH


class Place:
    def __init__(self, depth):
        self.depth = depth
        e, t = lax.axis_index("ep"), lax.axis_index("tp")
        self.z, self.x, self.y, self.c = e // 2, e % 2, t // 2, t % 2

    def device(self, k=0, dx=0, dy=0, dc=0):
        ep = (self.z + k) % self.depth * 2 + (self.x + dx) % 2
        tp = (self.y + dy) % 2 * 2 + (self.c + dc) % 2
        return ep, tp

    def block(self, k=0, dx=0, dy=0, dc=0):
        ep, tp = self.device(k, dx, dy, dc)
        return ep * 4 + tp

    def greet(self):
        barrier = pltpu.get_barrier_semaphore()
        near = [self.device(k=k) for k in range(1, self.depth)]
        near += [self.device(dx=1), self.device(dy=1), self.device(dc=1)]
        for who in near:
            pl.semaphore_signal(barrier, inc=1, device_id=who, device_id_type=MESH)
        pl.semaphore_wait(barrier, len(near))


def gather_kernel(depth, own, out, lane_recv, pair_recv, lane_send, pair_send, own_sem):
    here = Place(depth)
    half = own.shape[0] // 2
    sent = []

    def piece(k, dx, dy, part):
        rows = pl.ds(part * half, half)
        if (k, dx, dy) == (0, 0, 0):
            return own.at[rows]
        return out.at[here.block(k, dx, dy), rows]

    def lane_slot(k, dx, dy):
        ep, tp = here.device(k, dx, dy)
        return ep * 2 + tp // 2

    def push(k, dx, dy, part, to):
        rows = pl.ds(part * half, half)
        copy = pltpu.make_async_remote_copy(
            src_ref=piece(k, dx, dy, part), dst_ref=out.at[here.block(k, dx, dy), rows],
            send_sem=lane_send.at[len(sent)], recv_sem=lane_recv.at[lane_slot(k, dx, dy), part],
            device_id=to, device_id_type=MESH)
        copy.start()
        sent.append(copy)

    def pair(k, dx, dy, part):
        rows = pl.ds(part * half, half)
        slot = lane_slot(k, dx, dy)
        copy = pltpu.make_async_remote_copy(
            src_ref=piece(k, dx, dy, part), dst_ref=out.at[here.block(k, dx, dy), rows],
            send_sem=pair_send.at[slot, part], recv_sem=pair_recv.at[slot, part],
            device_id=here.device(dc=1), device_id_type=MESH)
        copy.start()

    def landed(k, dx, dy, part, to):
        rows = pl.ds(part * half, half)
        ref = out.at[here.block(k, dx, dy), rows]
        pltpu.make_async_remote_copy(
            src_ref=ref, dst_ref=ref, send_sem=lane_send.at[0],
            recv_sem=lane_recv.at[lane_slot(k, dx, dy), part],
            device_id=to, device_id_type=MESH).wait_recv()

    here.greet()
    over_x, over_y = here.device(dx=1), here.device(dy=1)
    for k in range(1, depth):
        for part in (0, 1):
            push(0, 0, 0, part, here.device(k=depth - k))
    store = pltpu.make_async_copy(own, out.at[here.block()], own_sem)
    store.start()
    for k in range(depth):
        if k:
            landed(k, 0, 0, 0, here.device(k=k))
            landed(k, 0, 0, 1, here.device(k=k))
        push(k, 0, 0, 0, over_x)
        push(k, 0, 0, 1, over_y)
        push(k, 0, 0, 0, over_y)
        push(k, 0, 0, 1, over_x)
        pair(k, 0, 0, 0)
        pair(k, 0, 0, 1)
        landed(k, 1, 0, 0, over_x)
        push(k, 1, 0, 0, over_y)
        pair(k, 1, 0, 0)
        landed(k, 0, 1, 1, over_y)
        push(k, 0, 1, 1, over_x)
        pair(k, 0, 1, 1)
    for k in range(depth):
        landed(k, 0, 1, 0, over_y)
        pair(k, 0, 1, 0)
        landed(k, 1, 0, 1, over_x)
        pair(k, 1, 0, 1)
        landed(k, 1, 1, 0, over_y)
        pair(k, 1, 1, 0)
        landed(k, 1, 1, 1, over_x)
        pair(k, 1, 1, 1)
    store.wait()
    for copy in sent:
        copy.wait_send()
    for k in range(depth):
        for dx in (0, 1):
            for dy in (0, 1):
                slot = lane_slot(k, dx, dy)
                for part in (0, 1):
                    rows = pl.ds(part * half, half)
                    copy = pltpu.make_async_remote_copy(
                        src_ref=piece(k, dx, dy, part),
                        dst_ref=out.at[here.block(k, dx, dy, 1), rows],
                        send_sem=pair_send.at[slot, part], recv_sem=pair_recv.at[slot, part],
                        device_id=here.device(dc=1), device_id_type=MESH)
                    copy.wait_send()
                    copy.wait_recv()


def gather_all(tokens, ep_count, tp_count):
    rows, width = tokens.shape
    depth = ep_count // 2
    blocks = ep_count * tp_count
    sends = 2 * (depth - 1) + 6 * depth
    dma = pltpu.SemaphoreType.DMA
    return pl.pallas_call(
        functools.partial(gather_kernel, depth),
        out_shape=jax.ShapeDtypeStruct((blocks, rows, width), tokens.dtype),
        in_specs=[pl.BlockSpec(memory_space=pltpu.VMEM)],
        out_specs=pl.BlockSpec(memory_space=pl.ANY),
        scratch_shapes=[dma((blocks // 2, 2)), dma((blocks // 2, 2)), dma((sends,)),
                        dma((blocks // 2, 2)), dma(())],
        compiler_params=pltpu.CompilerParams(collective_id=0, has_side_effects=True),
    )(tokens)


def scatter_kernel(depth, part_ref, out, acc, inc, from_y, from_x, last_x, last_y, from_z,
                   load_sem, pair_send, pair_recv, send_sem, recv_sem):
    here = Place(depth)
    rows = out.shape[0]
    half = rows // 2
    low, high = pl.ds(0, half), pl.ds(half, half)
    order = list(range(1, depth)) + [0]
    spread = ((1, 1), (0, 1), (1, 0), (0, 0))
    over_x, over_y = here.device(dx=1), here.device(dy=1)
    sent = []
    loads, pairs = {}, {}
    cell = lambda k, dx, dy: (k * 2 + dx) * 2 + dy

    def add(at, part, got):
        acc[at, part] = (acc[at, part].astype(jnp.float32) + got.astype(jnp.float32)).astype(acc.dtype)

    def send(src, dst, to):
        copy = pltpu.make_async_remote_copy(
            src_ref=src, dst_ref=dst, send_sem=send_sem.at[len(sent)],
            recv_sem=recv_sem.at[len(sent)], device_id=to, device_id_type=MESH)
        copy.start()
        sent.append(copy)
        return copy

    here.greet()
    for k in order:
        for dx, dy in spread:
            i = cell(k, dx, dy)
            pairs[i] = pltpu.make_async_remote_copy(
                src_ref=part_ref.at[here.block(k, dx, dy, 1)], dst_ref=inc.at[i],
                send_sem=pair_send.at[i], recv_sem=pair_recv.at[i],
                device_id=here.device(dc=1), device_id_type=MESH)
            pairs[i].start()
            loads[i] = pltpu.make_async_copy(
                part_ref.at[here.block(k, dx, dy)], acc.at[i], load_sem.at[i])
            loads[i].start()

    wait_for = {}

    def first(k):
        for dx, dy in spread:
            i = cell(k, dx, dy)
            loads[i].wait()
            pairs[i].wait_recv()
            add(i, pl.ds(0, rows), inc[i])
            if dy:
                wait_for["y", k, dx] = send(acc.at[i, low], from_y.at[k * 2 + dx], over_y)
            if dx:
                wait_for["x", k, dy] = send(acc.at[i, high], from_x.at[k * 2 + dy], over_x)

    def second(k):
        wait_for["y", k, 1].wait_recv()
        add(cell(k, 1, 0), low, from_y[k * 2 + 1])
        wait_for["lx", k] = send(acc.at[cell(k, 1, 0), low], last_x.at[k], over_x)
        wait_for["x", k, 1].wait_recv()
        add(cell(k, 0, 1), high, from_x[k * 2 + 1])
        wait_for["ly", k] = send(acc.at[cell(k, 0, 1), high], last_y.at[k], over_y)
        wait_for["y", k, 0].wait_recv()
        add(cell(k, 0, 0), low, from_y[k * 2])
        wait_for["x", k, 0].wait_recv()
        add(cell(k, 0, 0), high, from_x[k * 2])

    def third(k):
        wait_for["lx", k].wait_recv()
        add(cell(k, 0, 0), low, last_x[k])
        wait_for["ly", k].wait_recv()
        add(cell(k, 0, 0), high, last_y[k])
        if k:
            wait_for["z", k] = send(acc.at[cell(k, 0, 0)], from_z.at[k - 1], here.device(k=k))

    for i in range(depth + 2):
        if i < depth:
            first(order[i])
        if 0 <= i - 1 < depth:
            second(order[i - 1])
        if 0 <= i - 2:
            third(order[i - 2])
    total = acc[0].astype(jnp.float32)
    for k in range(1, depth):
        wait_for["z", k].wait_recv()
        total = total + from_z[k - 1].astype(jnp.float32)
    out[...] = total.astype(out.dtype)
    for copy in sent:
        copy.wait_send()
    for copy in pairs.values():
        copy.wait_send()


def scatter_sum(partial, ep_count):
    blocks, rows, width = partial.shape
    depth = ep_count // 2
    lane, half = blocks // 2, rows // 2
    sends = 6 * depth + depth - 1
    dma, kind = pltpu.SemaphoreType.DMA, partial.dtype
    return pl.pallas_call(
        functools.partial(scatter_kernel, depth),
        out_shape=jax.ShapeDtypeStruct((rows, width), kind),
        in_specs=[pl.BlockSpec(memory_space=pl.ANY)],
        out_specs=pl.BlockSpec(memory_space=pltpu.VMEM),
        scratch_shapes=[
            pltpu.VMEM((lane, rows, width), kind), pltpu.VMEM((lane, rows, width), kind),
            pltpu.VMEM((2 * depth, half, width), kind), pltpu.VMEM((2 * depth, half, width), kind),
            pltpu.VMEM((depth, half, width), kind), pltpu.VMEM((depth, half, width), kind),
            pltpu.VMEM((depth - 1, rows, width), kind),
            dma((lane,)), dma((lane,)), dma((lane,)), dma((sends,)), dma((sends,)),
        ],
        compiler_params=pltpu.CompilerParams(
            collective_id=1, has_side_effects=True, vmem_limit_bytes=48 * 1024 * 1024),
    )(partial)


def local(tokens, expert_ids, combine_weights, gate_weight, up_weight, down_weight):
    ep_count = lax.axis_size("ep")
    tp_count = lax.axis_size("tp")
    exp_local = gate_weight.shape[0]
    experts = exp_local * ep_count
    tok_rows = expert_ids.shape[0]
    top_count = expert_ids.shape[1]
    capacity = 2 * tok_rows * top_count // experts
    feat_width = tokens.shape[1]
    ff_width = gate_weight.shape[2]
    width = feat_width * tp_count
    f32, bf16 = jnp.float32, jnp.bfloat16

    ids_all = lax.all_gather(expert_ids.T, "ep")
    weights_all = lax.all_gather(combine_weights.T, "ep")
    first = lax.axis_index("ep") * exp_local
    mine = first + jnp.arange(exp_local, dtype=jnp.int32)
    hit = ids_all[:, None, :, :] == mine[None, :, None, None]
    chosen = jnp.any(hit, axis=2)
    weight = jnp.sum(jnp.where(hit, weights_all[:, None, :, :], 0.0), axis=2)

    ahead = jnp.triu(jnp.ones((tok_rows, tok_rows), bf16), 1)
    slot = lax.dot_general(
        chosen.reshape(-1, tok_rows).astype(bf16), ahead, (((1,), (0,)), ((), ())),
        preferred_element_type=f32,
    ).astype(jnp.int32).reshape(chosen.shape)
    place = jnp.where(chosen, slot, -1)
    take = place[:, :, None, :] == jnp.arange(capacity, dtype=jnp.int32)[None, None, :, None]
    slot_weight = jnp.sum(jnp.where(take, weight[:, :, None, :], 0.0), axis=3)
    take = take.astype(bf16)

    paired = tp_count == 2 * 2 and ep_count % 2 == 0
    spread = gather_all(tokens, ep_count, tp_count) if paired else lax.all_gather(
        tokens, ("ep", "tp")
    )
    gathered = spread.reshape(
        ep_count, tp_count, tok_rows, feat_width
    )
    routed = jnp.einsum(
        "sect,sjtf->escjf", take, gathered, preferred_element_type=f32
    ).astype(bf16)
    rows = routed.reshape(exp_local, ep_count * capacity, width)
    gate_new = jnp.einsum("erd,edf->erf", rows, gate_weight, preferred_element_type=f32)
    up_new = jnp.einsum("erd,edf->erf", rows, up_weight, preferred_element_type=f32)
    row_weight = slot_weight.transpose(1, 0, 2).reshape(exp_local, ep_count * capacity, 1)
    hidden = (activate(gate_new, up_new) * row_weight).astype(bf16)
    expert_out = jnp.einsum(
        "erf,efd->erd", hidden, down_weight, preferred_element_type=f32
    ).astype(bf16)
    expert_out = expert_out.reshape(exp_local, ep_count, capacity, tp_count, feat_width)
    partial = jnp.einsum(
        "sect,escjf->sjtf", take, expert_out, preferred_element_type=f32
    ).astype(bf16)
    partial = partial.reshape(ep_count * tp_count, tok_rows, feat_width)
    if paired:
        return scatter_sum(partial, ep_count)
    mixed = lax.psum_scatter(partial, ("ep", "tp"), scatter_dimension=0, tiled=True)
    return mixed.reshape(tok_rows, feat_width)


def solution(mesh):
    in_specs = (
        P("ep", "tp"),
        P("ep", None),
        P("ep", None),
        P("ep", None, "tp"),
        P("ep", None, "tp"),
        P("ep", "tp", None),
    )
    out_specs = P("ep", "tp")
    return jax.shard_map(local, mesh=mesh, in_specs=in_specs, out_specs=out_specs, check_vma=False)
```

profile of v0, /device:TPU:0, one launch (start us, length us, event | category | flops | bytes accessed | tf_op | source)
XLA Modules:
  0.0 342.3 jit_solution(12794418423876645274)
XLA Ops:
  0.0 32.5 %all-gather.2 = s32[8,4,256]{2,1,0:T(4,128)S(1)} all-gather(s32[1,4,256]{2,1,0:T(4,128)} %bitcast.55), channel_id=2, replica_groups=mesh['ep'=8,'tp'=4] {'ep'}, dimensions={0}, use_global_device_ids=true | all-gather | bytes 36864 | tf_op jit(solution)/shard_map/all_gather | solution.py:274
  32.6 0.1 compare_reduce_fusion
  32.7 0.1 convolution_convert_fusion.1
  32.9 30.7 %all-gather.3 = f32[8,4,256]{2,1,0:T(4,128)S(1)} all-gather(f32[1,4,256]{2,1,0:T(4,128)} %bitcast.56), channel_id=3, replica_groups=mesh['ep'=8,'tp'=4] {'ep'}, dimensions={0}, use_global_device_ids=true | all-gather | bytes 36864 | tf_op jit(solution)/shard_map/all_gather | solution.py:275
  63.7 0.1 fusion.16
  63.7 0.4 select_reduce_fusion
  64.2 1.9 copy.28.own
  66.1 65.2 %shard_map.64 = bf16[32,256,720]{2,1,0:T(8,128)(2,1)} custom-call(bf16[256,720]{1,0:T(8,128)(2,1)} %copy.28.own), custom_call_target="tpu_custom_call" | custom-call | tf_op jit(solution)/shard_map/pallas_call | solution.py:139
  131.3 15.0 %convert_bitcast_fusion = bf16[2,8,128,4,720]{2,4,3,0,1:T(8,128)(2,1)} fusion(bf16[8,4,256,720,1]{3,2,1,4,0:T(8,128)(2,1)} %bitcast.50, s32[8,2,256]{2,1,0:T(2,128)S(1)} %copy.27), kind=kOutput, calls=%fused_computation.4 | convolution fusion | flops 3026321408 | bytes 23609344 | tf_op jit(solution)/shard_map/sect,sjtf->escjf/dot_general | solution.py:299
  146.4 24.3 %copy.30 = bf16[2,8,128,4,720]{2,1,4,3,0:T(8,128)(2,1)} copy(bf16[2,8,128,4,720]{2,4,3,0,1:T(8,128)(2,1)} %convert_bitcast_fusion) | data formatting | bytes 23592960 | tf_op jit(solution)/shard_map/convert_element_type | solution.py:301
  170.7 18.5 %reshape.37 = bf16[2,1024,2880]{1,2,0:T(8,128)(2,1)} reshape(bf16[2,8,128,4,720]{2,1,4,3,0:T(8,128)(2,1)} %copy.30) | data formatting | bytes 23592960 | tf_op jit(solution)/shard_map/reshape | solution.py:302
  189.2 16.2 %fusion.25 = f32[2,1024,720]{1,2,0:T(8,128)} fusion(bf16[2,2880,720]{1,2,0:T(8,128)(2,1)} %param.9, bf16[2,1024,2880]{1,2,0:T(8,128)(2,1)} %reshape.37), kind=kOutput, calls=%fused_computation.31 | convolution fusion | flops 8493465600 | bytes 25989120 | tf_op jit(solution)/shard_map/erd,edf->erf/dot_general | solution.py:303
  205.3 27.2 %convolution_convert_fusion = bf16[2,1024,2880]{1,2,0:T(8,128)(2,1)} fusion(bf16[2,720,2880]{2,1,0:T(8,128)(2,1)} %param.11, f32[2,1024,720]{1,2,0:T(8,128)} %fusion.25, f32[2,1024]{1,0:T(2,128)S(1)} %bitcast.54, bf16[2,2880,720]{1,2,0:T(8,128)(2,1)} %param.10, bf16[2,1024,2880]{1,2,0:T(8,128)(2,1)} %reshape.37), kind=kOutput, calls=%fused_computation.5 | convolution fusion | flops 17006100480 | bytes 46088192 | tf_op jit(solution)/shard_map/erf,efd->erd/dot_general | solution.py:307
  232.5 11.3 %copy.42 = bf16[720,8,8,128]{3,2,1,0:T(8,128)(2,1)} copy(bf16[720,8,8,128]{3,1,2,0:T(8,128)(2,1)} %bitcast.53) | data formatting | bytes 23592960
  243.8 14.2 %fusion = bf16[8,4,256,720]{2,3,1,0:T(8,128)(2,1)} fusion(bf16[2,8,128,4,720]{2,1,4,3,0:T(8,128)(2,1)} %bitcast.52, s32[8,2,256]{2,1,0:T(2,128)S(1)} %copy.27), kind=kOutput, calls=%fused_computation.1 | convolution fusion | flops 3026321408 | bytes 23609344 | tf_op jit(solution)/shard_map/sect,escjf->sjtf/dot_general | solution.py:311
  258.0 16.3 %copy.34 = bf16[8,4,256,720]{3,2,1,0:T(8,128)(2,1)} copy(bf16[8,4,256,720]{2,3,1,0:T(8,128)(2,1)} %fusion) | data formatting | bytes 23592960 | tf_op jit(solution)/shard_map/convert_element_type | solution.py:313
  274.3 67.1 %shard_map.65 = bf16[256,720]{1,0:T(8,128)(2,1)S(1)} custom-call(bf16[32,256,720]{2,1,0:T(8,128)(2,1)} %bitcast.51), custom_call_target="tpu_custom_call" | custom-call | tf_op jit(solution)/shard_map/pallas_call | solution.py:244
  341.4 0.9 copy.35
  (9 shorter events, 0.1 us)
where the time goes:
time: 344 us; the launch traced here: 342 us
  Pallas kernels  132 us (38%)
  local copies, waits for them, and re-layouts  73.3 us (21%)
  matrix products  72.7 us (21%)
  blocking collectives  63.3 us (18%)
    pallas_call x1, Pallas kernels, scatter_sum(): pl.pallas_call(functools.partial(scatter_kernel, depth), out_shape=jax.Sh...  67.1 us
    pallas_call x1, Pallas kernels, gather_all(): pl.pallas_call(functools.partial(gather_kernel, depth), out_shape=jax.Sha...  65.2 us
    all_gather x1, blocking collectives, local(): ids_all = lax.all_gather(expert_ids.T, 'ep')  32.5 us
    all_gather x1, blocking collectives, local(): weights_all = lax.all_gather(combine_weights.T, 'ep')  30.7 us
    dot_general x1, matrix products, local(): jnp.einsum('erf,efd->erd', hidden, down_weight, preferred_element_type=f32)  27.2 us
    convert_element_type x1, local copies, waits for them, and re-layouts, local(): routed = jnp.einsum('sect,sjtf->escjf', take, gathered, preferred_element...  24.3 us
    reshape x1, local copies, waits for them, and re-layouts, local(): rows = routed.reshape(exp_local, ep_count * capacity, width)  18.5 us
    convert_element_type x1, local copies, waits for them, and re-layouts, local(): partial = jnp.einsum('sect,escjf->sjtf', take, expert_out, preferred_elem...  16.3 us

commit v1 on v0

--- a/solution.py
+++ b/solution.py
@@ -258,6 +258,379 @@
     )(partial)
 
 
+def act_weighted(gate_acc, up_acc, weight):
+    return (activate(gate_acc, up_acc) * weight).astype(jnp.bfloat16)
+
+
+PUSHES = (((0, 0), 0, "x"), ((0, 0), 1, "y"), ((0, 0), 0, "y"), ((0, 0), 1, "x"),
+          ((1, 0), 0, "y"), ((0, 1), 1, "x"))
+
+
+class Grid:
+    def __init__(self):
+        e, t = lax.axis_index("ep"), lax.axis_index("tp")
+        self.ep, self.tp = e, t
+        self.z, self.x, self.y, self.c = e // 2, e % 2, t // 2, t % 2
+
+    def device(self, k=0, dx=0, dy=0, dc=0):
+        z = (self.z // 2 + k // 2) % 2 * 2 + (self.z % 2 + k % 2) % 2
+        return z * 2 + (self.x + dx) % 2, (self.y + dy) % 2 * 2 + (self.c + dc) % 2
+
+
+def fused_kernel(tokens, meta, gate, up, down, out, buf, inc, from_y, from_x, last_x, last_y,
+                 from_z, wide, deep, rows, hid, take, back, weigh, place, metas,
+                 own_sem, w_sem, meta_send, meta_recv, z_send, z_recv, lane_send, lane_recv,
+                 pair_send, pair_recv, sp_send, sp_recv, sx_send, sx_recv, sz_send, sz_recv):
+    f32, bf16 = jnp.float32, jnp.bfloat16
+    here = Grid()
+    depth = from_z.shape[0] + 1
+    tok, feat = buf.shape[1], buf.shape[2]
+    half = tok // 2
+    experts, cap = rows.shape[1], rows.shape[2]
+    lanes = rows.shape[3] // 4
+    ff = hid.shape[1]
+    width = deep.shape[2]
+    low, high = pl.ds(0, half), pl.ds(half, half)
+    parts = (low, high)
+    over = {"x": here.device(dx=1), "y": here.device(dy=1)}
+    partner = here.device(dc=1)
+
+    def cell(k, dx, dy, dc):
+        return k * 8 + dx * 4 + dy * 2 + dc
+
+    def remote(src, dst, send, recv, to):
+        return pltpu.make_async_remote_copy(
+            src_ref=src, dst_ref=dst, send_sem=send, recv_sem=recv,
+            device_id=to, device_id_type=MESH)
+
+    def z_push(k, p):
+        return remote(tokens.at[parts[p]], buf.at[cell(k, 0, 0, 0), parts[p]],
+                      z_send.at[k, p], z_recv.at[k, p], here.device(k=k))
+
+    def lane_push(k, n):
+        (dx, dy), p, axis = PUSHES[n]
+        to = (1 - dx, dy) if axis == "x" else (dx, 1 - dy)
+        return remote(buf.at[cell(k, dx, dy, 0), parts[p]], buf.at[cell(k, *to, 0), parts[p]],
+                      lane_send.at[k, n], lane_recv.at[k, n], over[axis])
+
+    def pair(k, dx, dy, p):
+        n = (dx * 2 + dy) * 2 + p
+        return remote(buf.at[cell(k, dx, dy, 0), parts[p]], buf.at[cell(k, dx, dy, 1), parts[p]],
+                      pair_send.at[k, n], pair_recv.at[k, n], partner)
+
+    def meta_push(k, dx):
+        n = k * 2 + dx
+        return remote(meta, metas.at[n], meta_send.at[n], meta_recv.at[n], here.device(k=k, dx=dx))
+
+    def gather_a(k):
+        for n in range(4):
+            lane_push(k, n).start()
+        pair(k, 0, 0, 0).start()
+        pair(k, 0, 0, 1).start()
+
+    def column(k):
+        z_push(k, 0).wait_recv()
+        z_push(k, 1).wait_recv()
+        gather_a(k)
+
+    def gather_b(k):
+        lane_push(k, 0).wait_recv()
+        lane_push(k, 4).start()
+        pair(k, 1, 0, 0).start()
+        lane_push(k, 1).wait_recv()
+        lane_push(k, 5).start()
+        pair(k, 0, 1, 1).start()
+
+    def gather_c(k, first):
+        if first:
+            lane_push(k, 2).wait_recv()
+            pair(k, 0, 1, 0).start()
+            lane_push(k, 3).wait_recv()
+            pair(k, 1, 0, 1).start()
+        else:
+            lane_push(k, 4).wait_recv()
+            pair(k, 1, 1, 0).start()
+            lane_push(k, 5).wait_recv()
+            pair(k, 1, 1, 1).start()
+
+    def gather_d(k):
+        for dx in (0, 1):
+            for dy in (0, 1):
+                for p in (0, 1):
+                    pair(k, dx, dy, p).wait_recv()
+
+    def gather_sent(k):
+        for n in range(6):
+            lane_push(k, n).wait_send()
+        for dx in (0, 1):
+            for dy in (0, 1):
+                for p in (0, 1):
+                    pair(k, dx, dy, p).wait_send()
+
+    def give(k, dx, dy):
+        n = dx * 2 + dy
+        return remote(buf.at[cell(k, dx, dy, 1)], inc.at[k * 4 + n],
+                      sp_send.at[k, n], sp_recv.at[k, n], partner)
+
+    def hop(k, n):
+        src, dst, axis = (
+            (buf.at[cell(k, 1, 1, 0), low], from_y.at[k * 2 + 1], "y"),
+            (buf.at[cell(k, 0, 1, 0), low], from_y.at[k * 2], "y"),
+            (buf.at[cell(k, 1, 1, 0), high], from_x.at[k * 2 + 1], "x"),
+            (buf.at[cell(k, 1, 0, 0), high], from_x.at[k * 2], "x"),
+            (buf.at[cell(k, 1, 0, 0), low], last_x.at[k], "x"),
+            (buf.at[cell(k, 0, 1, 0), high], last_y.at[k], "y"))[n]
+        return remote(src, dst, sx_send.at[k, n], sx_recv.at[k, n], over[axis])
+
+    def home(k):
+        return remote(buf.at[cell(k, 0, 0, 0)], from_z.at[k - 1],
+                      sz_send.at[k], sz_recv.at[k], here.device(k=k))
+
+    def add(at, part, got):
+        buf[at, part] = (buf[at, part].astype(f32) + got.astype(f32)).astype(bf16)
+
+    def scatter_b(k):
+        for dx, dy in ((1, 1), (0, 1), (1, 0), (0, 0)):
+            give(k, dx, dy).wait_recv()
+            add(cell(k, dx, dy, 0), pl.ds(0, tok), inc[k * 4 + dx * 2 + dy])
+            if dy:
+                hop(k, 1 - dx).start()
+            if dx:
+                hop(k, 3 - dy).start()
+
+    def scatter_c(k):
+        hop(k, 0).wait_recv()
+        add(cell(k, 1, 0, 0), low, from_y[k * 2 + 1])
+        hop(k, 4).start()
+        hop(k, 2).wait_recv()
+        add(cell(k, 0, 1, 0), high, from_x[k * 2 + 1])
+        hop(k, 5).start()
+        hop(k, 1).wait_recv()
+        add(cell(k, 0, 0, 0), low, from_y[k * 2])
+        hop(k, 3).wait_recv()
+        add(cell(k, 0, 0, 0), high, from_x[k * 2])
+
+    def scatter_d(k):
+        hop(k, 4).wait_recv()
+        add(cell(k, 0, 0, 0), low, last_x[k])
+        hop(k, 5).wait_recv()
+        add(cell(k, 0, 0, 0), high, last_y[k])
+
+    own = pltpu.make_async_copy(tokens, buf.at[cell(0, 0, 0, 0)], own_sem)
+    own.start()
+    barrier = pltpu.get_barrier_semaphore()
+    near = [here.device(k=k, dx=dx) for k in range(depth) for dx in (0, 1) if k or dx]
+    near += [over["y"], partner]
+    for who in near:
+        pl.semaphore_signal(barrier, inc=1, device_id=who, device_id_type=MESH)
+    pl.semaphore_wait(barrier, len(near))
+    for k in range(depth):
+        for dx in (0, 1):
+            if k or dx:
+                meta_push(k, dx).start()
+    for k in range(1, depth):
+        z_push(k, 0).start()
+        z_push(k, 1).start()
+    own.wait()
+    gather_a(0)
+    loads = []
+    for e in range(experts):
+        for side, ref in enumerate((gate, up)):
+            for j in range(4):
+                loads.append(pltpu.make_async_copy(
+                    ref.at[e, pl.ds(j * feat, feat)], wide.at[side, e, pl.ds(j * lanes, feat)],
+                    w_sem.at[len(loads)]))
+        loads.append(pltpu.make_async_copy(down.at[e], deep.at[e], w_sem.at[len(loads)]))
+    for load in loads:
+        load.start()
+    metas[0] = meta[...]
+    place[...] = jnp.zeros(place.shape, f32)
+    for j in range(4):
+        edge = pl.ds(j * lanes + feat, lanes - feat)
+        for e in range(experts):
+            for side in (0, 1):
+                wide[side, e, edge, :] = jnp.zeros((lanes - feat, ff), bf16)
+            for dx in (0, 1):
+                rows[dx, e, :, edge] = jnp.zeros((cap, lanes - feat), bf16)
+    gather_b(0)
+    column(1)
+    gather_c(0, True)
+    gather_c(0, False)
+    for load in loads:
+        load.wait()
+
+    ahead = (lax.broadcasted_iota(jnp.int32, (tok, tok), 0)
+             < lax.broadcasted_iota(jnp.int32, (tok, tok), 1)).astype(f32).astype(bf16)
+    slot_row = lax.broadcasted_iota(jnp.int32, (cap, tok), 0).astype(f32)
+    slot_col = lax.broadcasted_iota(jnp.int32, (tok, cap), 1).astype(f32)
+    row_at = lax.broadcasted_iota(jnp.int32, (8, tok), 0)
+
+    def masks(k):
+        picked = jnp.zeros((8, tok), f32)
+        weights = []
+        for dx in (0, 1):
+            info = metas[k * 2 + dx]
+            for e in range(experts):
+                mine = (here.ep * experts + e).astype(f32)
+                hit = (info[0:4] == mine).astype(f32)
+                chosen = jnp.sum(hit, axis=0, keepdims=True)
+                weights.append(jnp.sum(hit * info[4:8], axis=0, keepdims=True))
+                picked = jnp.where(row_at == dx * experts + e, chosen, picked)
+        slot = jnp.dot(picked.astype(bf16), ahead, preferred_element_type=f32)
+        slot = jnp.where(picked > 0.5, slot, -1.0)
+        place[0:8, :] = slot
+        turned = jnp.transpose(place[...])
+        for dx in (0, 1):
+            for e in range(experts):
+                n = dx * experts + e
+                at = pl.ds(e * cap, cap)
+                hot = (slot_row == slot[n:n + 1, :]).astype(f32)
+                take[dx, at, :] = hot.astype(bf16)
+                held = jnp.sum(hot * weights[n], axis=1, keepdims=True)
+                weigh[e, pl.ds(dx * cap, cap), :] = jnp.broadcast_to(held, (cap, 128))
+                back[dx, :, at] = (slot_col == turned[:, n:n + 1]).astype(f32).astype(bf16)
+
+    def block(k, dx, j):
+        return cell(k, dx, (here.y + j // 2) % 2, (here.c + j % 2) % 2)
+
+    def dispatch(k):
+        for dx in (0, 1):
+            for j in range(4):
+                got = jnp.dot(take[dx], buf[block(k, dx, j)], preferred_element_type=f32)
+                rows[dx, :, :, pl.ds(j * lanes, feat)] = got.astype(bf16).reshape(experts, cap, feat)
+
+    def enter(e):
+        held = rows[:, e].reshape(2 * cap, 4 * lanes)
+        for n in range(0, ff, 256):
+            at = pl.ds(n, min(256, ff - n))
+            g = jnp.dot(held, wide[0, e, :, at], preferred_element_type=f32)
+            u = jnp.dot(held, wide[1, e, :, at], preferred_element_type=f32)
+            hid[:, at] = act_weighted(g, u, weigh[e, :, 0:1])
+
+    def leave(e):
+        for n in range(0, width, 512):
+            size = min(512, width - n)
+            got = jnp.dot(hid[...], deep[e, :, pl.ds(n, size)], preferred_element_type=f32)
+            rows[:, e, :, pl.ds(n, size)] = got.astype(bf16).reshape(2, cap, size)
+
+    def combine(k, dx):
+        for j in range(4):
+            part = rows[dx, :, :, pl.ds(j * feat, feat)].reshape(experts * cap, feat)
+            got = jnp.dot(back[dx], part, preferred_element_type=f32)
+            buf[block(k, dx, j)] = got.astype(bf16)
+
+    def plane(k, carry):
+        last = depth - 1
+        gather_d(k)
+
+        @pl.when(k > 0)
+        def _():
+            meta_push(k, 0).wait_recv()
+        meta_push(k, 1).wait_recv()
+        masks(k)
+        dispatch(k)
+
+        @pl.when(k < last)
+        def _():
+            gather_b(k + 1)
+        enter(0)
+
+        @pl.when(k < last - 1)
+        def _():
+            column(k + 2)
+
+        @pl.when(k > 1)
+        def _():
+            scatter_b(k - 1)
+        leave(0)
+        enter(1)
+
+        @pl.when(k < last)
+        def _():
+            gather_c(k + 1, True)
+        leave(1)
+        gather_sent(k)
+
+        @pl.when(k < last)
+        def _():
+            gather_c(k + 1, False)
+        for dx in (1, 0):
+            combine(k, dx)
+            give(k, dx, 1).start()
+            give(k, dx, 0).start()
+        return carry
+
+    lax.fori_loop(0, depth, plane, 0)
+
+    scatter_c(1)
+    scatter_b(3)
+    scatter_c(2)
+    scatter_d(1)
+    home(1).start()
+    scatter_b(0)
+    scatter_c(3)
+    scatter_d(2)
+    home(2).start()
+    scatter_c(0)
+    scatter_d(3)
+    home(3).start()
+    scatter_d(0)
+    total = buf[cell(0, 0, 0, 0)].astype(f32)
+    for k in range(1, depth):
+        home(k).wait_recv()
+        total = total + from_z[k - 1].astype(f32)
+    out[...] = total.astype(out.dtype)
+    for k in range(depth):
+        for dx in (0, 1):
+            if k or dx:
+                meta_push(k, dx).wait_send()
+            for dy in (0, 1):
+                give(k, dx, dy).wait_send()
+        for n in range(6):
+            hop(k, n).wait_send()
+        if k:
+            z_push(k, 0).wait_send()
+            z_push(k, 1).wait_send()
+            home(k).wait_send()
+
+
+def fused(tokens, expert_ids, combine_weights, gate_weight, up_weight, down_weight, depth, capacity):
+    tok, feat = tokens.shape
+    experts, width, ff = gate_weight.shape
+    f32, bf16 = jnp.float32, jnp.bfloat16
+    lanes = -(-feat // 128) * 128
+    half = tok // 2
+    meta = jnp.concatenate([expert_ids.T.astype(f32), combine_weights.T], axis=0)
+    dma = pltpu.SemaphoreType.DMA
+    any_space, vmem = pl.BlockSpec(memory_space=pl.ANY), pl.BlockSpec(memory_space=pltpu.VMEM)
+    loads = experts * 9
+    scratch = [
+        pltpu.VMEM((depth * 8, tok, feat), bf16), pltpu.VMEM((depth * 4, tok, feat), bf16),
+        pltpu.VMEM((depth * 2, half, feat), bf16), pltpu.VMEM((depth * 2, half, feat), bf16),
+        pltpu.VMEM((depth, half, feat), bf16), pltpu.VMEM((depth, half, feat), bf16),
+        pltpu.VMEM((depth - 1, tok, feat), bf16),
+        pltpu.VMEM((2, experts, 4 * lanes, ff), bf16), pltpu.VMEM((experts, ff, width), bf16),
+        pltpu.VMEM((2, experts, capacity, 4 * lanes), bf16),
+        pltpu.VMEM((2 * capacity, ff), bf16),
+        pltpu.VMEM((2, experts * capacity, tok), bf16), pltpu.VMEM((2, tok, experts * capacity), bf16),
+        pltpu.VMEM((experts, 2 * capacity, 128), f32), pltpu.VMEM((128, tok), f32),
+        pltpu.VMEM((depth * 2, 8, tok), f32),
+        dma(()), dma((loads,)), dma((depth * 2,)), dma((depth * 2,)),
+        dma((depth, 2)), dma((depth, 2)), dma((depth, 6)), dma((depth, 6)),
+        dma((depth, 8)), dma((depth, 8)), dma((depth, 4)), dma((depth, 4)),
+        dma((depth, 6)), dma((depth, 6)), dma((depth,)), dma((depth,)),
+    ]
+    return pl.pallas_call(
+        fused_kernel,
+        out_shape=jax.ShapeDtypeStruct((tok, feat), bf16),
+        in_specs=[any_space, vmem, any_space, any_space, any_space],
+        out_specs=vmem,
+        scratch_shapes=scratch,
+        compiler_params=pltpu.CompilerParams(
+            collective_id=0, has_side_effects=True, vmem_limit_bytes=63 * 1024 * 1024),
+    )(tokens, meta, gate_weight, up_weight, down_weight)
+
+
 def local(tokens, expert_ids, combine_weights, gate_weight, up_weight, down_weight):
     ep_count = lax.axis_size("ep")
     tp_count = lax.axis_size("tp")
@@ -270,6 +643,9 @@
     ff_width = gate_weight.shape[2]
     width = feat_width * tp_count
     f32, bf16 = jnp.float32, jnp.bfloat16
+    if (ep_count, tp_count, exp_local, top_count) == (8, 4, 2, 4) and capacity % 128 == 0:
+        return fused(tokens, expert_ids, combine_weights, gate_weight, up_weight, down_weight,
+                     ep_count // 2, capacity)
 
     ids_all = lax.all_gather(expert_ids.T, "ep")
     weights_all = lax.all_gather(combine_weights.T, "ep")

time: 344 us -> 159 us (0.46)
  the two profiles are of different devices: /device:TPU:0 before, /device:TPU:12 now
where the time goes in v1:
time: 159 us; the launch traced here: 158 us
  Pallas kernels  129 us (81%)
  local copies, waits for them, and re-layouts  27.2 us (17%)
  other arithmetic  1.98 us (1%)
    pallas_call x1, Pallas kernels, fused(): pl.pallas_call(fused_kernel, out_shape=jax.ShapeDtypeStruct((tok, feat),...  129 us
    unnamed x3, local copies, waits for them, and re-layouts  25.3 us

profile of v1, /device:TPU:12, one launch (start us, length us, event | category | flops | bytes accessed | tf_op | source)
XLA Modules:
  0.0 157.9 jit_solution(796146796908544952)
XLA Ops:
  0.0 0.7 convert_bitcast_fusion
  0.7 1.3 pad_maximum_fusion.meta
  2.0 1.9 %copy.7.tokens = bf16[256,720]{1,0:T(8,128)(2,1)} copy(bf16[256,720]{0,1:T(8,128)(2,1)} %param.6) | data formatting | bytes 737280 | tf_op args[0]
  3.9 11.8 %copy.8.gate = bf16[2,2880,720]{2,1,0:T(8,128)(2,1)} copy(bf16[2,2880,720]{1,2,0:T(8,128)(2,1)} %param.9) | data formatting | bytes 16588800 | tf_op args[3]
  15.7 11.7 %copy.9.up = bf16[2,2880,720]{2,1,0:T(8,128)(2,1)} copy(bf16[2,2880,720]{1,2,0:T(8,128)(2,1)} %param.10) | data formatting | bytes 16588800 | tf_op args[4]
  27.3 128.7 %shard_map.64 = bf16[256,720]{1,0:T(8,128)(2,1)} custom-call(bf16[256,720]{1,0:T(8,128)(2,1)} %copy.7.tokens, f32[8,256]{1,0:T(8,128)} %pad_maximum_fusion.meta, bf16[2,2880,720]{2,1,0:T(8,128)(2,1)} %copy.8.gate, bf16[2,2880,720]{2,1,0:T(8,128)(2,1)} %copy.9.up, bf16[2,720,2880]{2,1,0:T(8,128)(2,1)} %down.1), custom_call_target="tpu_custom_call" | custom-call | tf_op jit(solution)/shard_map/pallas_call | solution.py:623
  156.0 1.9 %copy.10 = bf16[256,720]{0,1:T(8,128)(2,1)} copy(bf16[256,720]{1,0:T(8,128)(2,1)} %shard_map.64) | data formatting | bytes 737280 | tf_op jit(solution)/shard_map/pallas_call | solution.py:623

commit v2 on v1

--- a/solution.py
+++ b/solution.py
@@ -262,6 +262,7 @@
     return (activate(gate_acc, up_acc) * weight).astype(jnp.bfloat16)
 
 
+STEP = 240
 PUSHES = (((0, 0), 0, "x"), ((0, 0), 1, "y"), ((0, 0), 0, "y"), ((0, 0), 1, "x"),
           ((1, 0), 0, "y"), ((0, 1), 1, "x"))
 
@@ -277,20 +278,18 @@
         return z * 2 + (self.x + dx) % 2, (self.y + dy) % 2 * 2 + (self.c + dc) % 2
 
 
-def fused_kernel(tokens, meta, gate, up, down, out, buf, inc, from_y, from_x, last_x, last_y,
-                 from_z, wide, deep, rows, hid, take, back, weigh, place, metas,
+def fused_kernel(tokens, ids, scales, gate, up, down, out, buf, inc, from_y, from_x, last_x, last_y,
+                 from_z, wide, deep, stage, rows, hid, take, back, weigh, place, all_ids, all_scales,
                  own_sem, w_sem, meta_send, meta_recv, z_send, z_recv, lane_send, lane_recv,
                  pair_send, pair_recv, sp_send, sp_recv, sx_send, sx_recv, sz_send, sz_recv):
     f32, bf16 = jnp.float32, jnp.bfloat16
     here = Grid()
     depth = from_z.shape[0] + 1
-    tok, feat = buf.shape[1], buf.shape[2]
-    half = tok // 2
-    experts, cap = rows.shape[1], rows.shape[2]
-    lanes = rows.shape[3] // 4
-    ff = hid.shape[1]
-    width = deep.shape[2]
-    low, high = pl.ds(0, half), pl.ds(half, half)
+    feat, tok = buf.shape[1], buf.shape[2]
+    experts, cap = wide.shape[1], rows.shape[2] // wide.shape[1]
+    ff, width = wide.shape[2], wide.shape[3]
+    half = from_y.shape[1]
+    low, high = pl.ds(0, half), pl.ds(half, feat - half)
     parts = (low, high)
     over = {"x": here.device(dx=1), "y": here.device(dy=1)}
     partner = here.device(dc=1)
@@ -318,9 +317,26 @@
         return remote(buf.at[cell(k, dx, dy, 0), parts[p]], buf.at[cell(k, dx, dy, 1), parts[p]],
                       pair_send.at[k, n], pair_recv.at[k, n], partner)
 
+    class Both:
+        def __init__(self, *copies):
+            self.copies = copies
+
+        def start(self):
+            for copy in self.copies:
+                copy.start()
+
+        def wait_recv(self):
+            for copy in self.copies:
+                copy.wait_recv()
+
+        def wait_send(self):
+            for copy in self.copies:
+                copy.wait_send()
+
     def meta_push(k, dx):
-        n = k * 2 + dx
-        return remote(meta, metas.at[n], meta_send.at[n], meta_recv.at[n], here.device(k=k, dx=dx))
+        n, to = k * 2 + dx, here.device(k=k, dx=dx)
+        return Both(remote(ids, all_ids.at[n], meta_send.at[0, n], meta_recv.at[0, n], to),
+                    remote(scales, all_scales.at[n], meta_send.at[1, n], meta_recv.at[1, n], to))
 
     def gather_a(k):
         for n in range(4):
@@ -392,7 +408,7 @@
     def scatter_b(k):
         for dx, dy in ((1, 1), (0, 1), (1, 0), (0, 0)):
             give(k, dx, dy).wait_recv()
-            add(cell(k, dx, dy, 0), pl.ds(0, tok), inc[k * 4 + dx * 2 + dy])
+            add(cell(k, dx, dy, 0), pl.ds(0, feat), inc[k * 4 + dx * 2 + dy])
             if dy:
                 hop(k, 1 - dx).start()
             if dx:
@@ -416,8 +432,11 @@
         hop(k, 5).wait_recv()
         add(cell(k, 0, 0, 0), high, last_y[k])
 
-    own = pltpu.make_async_copy(tokens, buf.at[cell(0, 0, 0, 0)], own_sem)
-    own.start()
+    own = [pltpu.make_async_copy(tokens, buf.at[cell(0, 0, 0, 0)], own_sem.at[0]),
+           pltpu.make_async_copy(ids, all_ids.at[0], own_sem.at[1]),
+           pltpu.make_async_copy(scales, all_scales.at[0], own_sem.at[2])]
+    for copy in own:
+        copy.start()
     barrier = pltpu.get_barrier_semaphore()
     near = [here.device(k=k, dx=dx) for k in range(depth) for dx in (0, 1) if k or dx]
     near += [over["y"], partner]
@@ -431,29 +450,34 @@
     for k in range(1, depth):
         z_push(k, 0).start()
         z_push(k, 1).start()
-    own.wait()
+    for copy in own:
+        copy.wait()
     gather_a(0)
-    loads = []
-    for e in range(experts):
-        for side, ref in enumerate((gate, up)):
-            for j in range(4):
-                loads.append(pltpu.make_async_copy(
-                    ref.at[e, pl.ds(j * feat, feat)], wide.at[side, e, pl.ds(j * lanes, feat)],
-                    w_sem.at[len(loads)]))
-        loads.append(pltpu.make_async_copy(down.at[e], deep.at[e], w_sem.at[len(loads)]))
+    loads = [pltpu.make_async_copy(ref.at[e], wide.at[side, e], w_sem.at[side, e])
+             for side, ref in enumerate((gate, up)) for e in range(experts)]
+    deeps = [pltpu.make_async_copy(down.at[e], stage, w_sem.at[2, e]) for e in range(experts)]
+    deeps[0].start()
     for load in loads:
         load.start()
-    metas[0] = meta[...]
     place[...] = jnp.zeros(place.shape, f32)
-    for j in range(4):
-        edge = pl.ds(j * lanes + feat, lanes - feat)
-        for e in range(experts):
-            for side in (0, 1):
-                wide[side, e, edge, :] = jnp.zeros((lanes - feat, ff), bf16)
-            for dx in (0, 1):
-                rows[dx, e, :, edge] = jnp.zeros((cap, lanes - feat), bf16)
+
+    def turn(e):
+        deeps[e].wait()
+        for n in range(0, width, 256):
+            size = min(256, width - n)
+            eye = (lax.broadcasted_iota(jnp.int32, (size, size), 0)
+                   == lax.broadcasted_iota(jnp.int32, (size, size), 1)).astype(f32).astype(bf16)
+            got = lax.dot_general(eye, stage[:, pl.ds(n, size)], (((1,), (1,)), ((), ())),
+                                  preferred_element_type=f32)
+            deep[e, pl.ds(n, size), :] = got.astype(bf16)
+        if e + 1 < experts:
+            deeps[e + 1].start()
+
+    turn(0)
     gather_b(0)
     column(1)
+    for e in range(1, experts):
+        turn(e)
     gather_c(0, True)
     gather_c(0, False)
     for load in loads:
@@ -467,28 +491,30 @@
 
     def masks(k):
         picked = jnp.zeros((8, tok), f32)
-        weights = []
+        known = jnp.zeros((8, tok), f32)
         for dx in (0, 1):
-            info = metas[k * 2 + dx]
+            named, scaled = all_ids[k * 2 + dx], all_scales[k * 2 + dx]
             for e in range(experts):
-                mine = (here.ep * experts + e).astype(f32)
-                hit = (info[0:4] == mine).astype(f32)
+                n = dx * experts + e
+                hit = (named == here.ep * experts + e).astype(f32)
                 chosen = jnp.sum(hit, axis=0, keepdims=True)
-                weights.append(jnp.sum(hit * info[4:8], axis=0, keepdims=True))
-                picked = jnp.where(row_at == dx * experts + e, chosen, picked)
+                picked = jnp.where(row_at == n, chosen, picked)
+                held = jnp.sum(hit * scaled, axis=0, keepdims=True)
+                known = jnp.where(row_at == 2 * experts + n, held, known)
         slot = jnp.dot(picked.astype(bf16), ahead, preferred_element_type=f32)
         slot = jnp.where(picked > 0.5, slot, -1.0)
-        place[0:8, :] = slot
+        place[0:8, :] = jnp.where(row_at < 2 * experts, slot, known)
         turned = jnp.transpose(place[...])
         for dx in (0, 1):
             for e in range(experts):
                 n = dx * experts + e
                 at = pl.ds(e * cap, cap)
-                hot = (slot_row == slot[n:n + 1, :]).astype(f32)
-                take[dx, at, :] = hot.astype(bf16)
-                held = jnp.sum(hot * weights[n], axis=1, keepdims=True)
-                weigh[e, pl.ds(dx * cap, cap), :] = jnp.broadcast_to(held, (cap, 128))
-                back[dx, :, at] = (slot_col == turned[:, n:n + 1]).astype(f32).astype(bf16)
+                take[dx, at, :] = (slot_row == slot[n:n + 1, :]).astype(f32).astype(bf16)
+                hot = (slot_col == turned[:, n:n + 1]).astype(f32)
+                back[dx, :, at] = hot.astype(bf16)
+                held = turned[:, 2 * experts + n:2 * experts + n + 1]
+                weigh[e, :, pl.ds(dx * cap, cap)] = jnp.broadcast_to(
+                    jnp.sum(hot * held, axis=0, keepdims=True), (8, cap))
 
     def block(k, dx, j):
         return cell(k, dx, (here.y + j // 2) % 2, (here.c + j % 2) % 2)
@@ -496,27 +522,29 @@
     def dispatch(k):
         for dx in (0, 1):
             for j in range(4):
-                got = jnp.dot(take[dx], buf[block(k, dx, j)], preferred_element_type=f32)
-                rows[dx, :, :, pl.ds(j * lanes, feat)] = got.astype(bf16).reshape(experts, cap, feat)
+                got = jnp.dot(buf[block(k, dx, j)], back[dx], preferred_element_type=f32)
+                rows[dx, pl.ds(j * feat, feat), :] = got.astype(bf16)
 
     def enter(e):
-        held = rows[:, e].reshape(2 * cap, 4 * lanes)
-        for n in range(0, ff, 256):
-            at = pl.ds(n, min(256, ff - n))
-            g = jnp.dot(held, wide[0, e, :, at], preferred_element_type=f32)
-            u = jnp.dot(held, wide[1, e, :, at], preferred_element_type=f32)
-            hid[:, at] = act_weighted(g, u, weigh[e, :, 0:1])
+        at = pl.ds(e * cap, cap)
+        held = jnp.concatenate([rows[0, :, at], rows[1, :, at]], axis=1)
+        for n in range(0, ff, STEP):
+            part = pl.ds(n, min(STEP, ff - n))
+            g = jnp.dot(wide[0, e, part, :], held, preferred_element_type=f32)
+            u = jnp.dot(wide[1, e, part, :], held, preferred_element_type=f32)
+            hid[part, :] = act_weighted(g, u, weigh[e, 0:1, :])
 
     def leave(e):
-        for n in range(0, width, 512):
-            size = min(512, width - n)
-            got = jnp.dot(hid[...], deep[e, :, pl.ds(n, size)], preferred_element_type=f32)
-            rows[:, e, :, pl.ds(n, size)] = got.astype(bf16).reshape(2, cap, size)
+        at = pl.ds(e * cap, cap)
+        for n in range(0, width, 2 * STEP):
+            part = pl.ds(n, min(2 * STEP, width - n))
+            got = jnp.dot(deep[e, part, :], hid[...], preferred_element_type=f32).astype(bf16)
+            rows[0, part, at] = got[:, 0:cap]
+            rows[1, part, at] = got[:, cap:2 * cap]
 
     def combine(k, dx):
         for j in range(4):
-            part = rows[dx, :, :, pl.ds(j * feat, feat)].reshape(experts * cap, feat)
-            got = jnp.dot(back[dx], part, preferred_element_type=f32)
+            got = jnp.dot(rows[dx, pl.ds(j * feat, feat), :], take[dx], preferred_element_type=f32)
             buf[block(k, dx, j)] = got.astype(bf16)
 
     def plane(k, carry):
@@ -597,38 +625,39 @@
 def fused(tokens, expert_ids, combine_weights, gate_weight, up_weight, down_weight, depth, capacity):
     tok, feat = tokens.shape
     experts, width, ff = gate_weight.shape
+    top = expert_ids.shape[1]
     f32, bf16 = jnp.float32, jnp.bfloat16
-    lanes = -(-feat // 128) * 128
-    half = tok // 2
-    meta = jnp.concatenate([expert_ids.T.astype(f32), combine_weights.T], axis=0)
+    half = -(-feat // 32) * 16
+    rest = feat - half
     dma = pltpu.SemaphoreType.DMA
-    any_space, vmem = pl.BlockSpec(memory_space=pl.ANY), pl.BlockSpec(memory_space=pltpu.VMEM)
-    loads = experts * 9
     scratch = [
-        pltpu.VMEM((depth * 8, tok, feat), bf16), pltpu.VMEM((depth * 4, tok, feat), bf16),
-        pltpu.VMEM((depth * 2, half, feat), bf16), pltpu.VMEM((depth * 2, half, feat), bf16),
-        pltpu.VMEM((depth, half, feat), bf16), pltpu.VMEM((depth, half, feat), bf16),
-        pltpu.VMEM((depth - 1, tok, feat), bf16),
-        pltpu.VMEM((2, experts, 4 * lanes, ff), bf16), pltpu.VMEM((experts, ff, width), bf16),
-        pltpu.VMEM((2, experts, capacity, 4 * lanes), bf16),
-        pltpu.VMEM((2 * capacity, ff), bf16),
+        pltpu.VMEM((depth * 8, feat, tok), bf16), pltpu.VMEM((depth * 4, feat, tok), bf16),
+        pltpu.VMEM((depth * 2, half, tok), bf16), pltpu.VMEM((depth * 2, rest, tok), bf16),
+        pltpu.VMEM((depth, half, tok), bf16), pltpu.VMEM((depth, rest, tok), bf16),
+        pltpu.VMEM((depth - 1, feat, tok), bf16),
+        pltpu.VMEM((2, experts, ff, width), bf16), pltpu.VMEM((experts, width, ff), bf16),
+        pltpu.VMEM((ff, width), bf16),
+        pltpu.VMEM((2, width, experts * capacity), bf16),
+        pltpu.VMEM((ff, 2 * capacity), bf16),
         pltpu.VMEM((2, experts * capacity, tok), bf16), pltpu.VMEM((2, tok, experts * capacity), bf16),
-        pltpu.VMEM((experts, 2 * capacity, 128), f32), pltpu.VMEM((128, tok), f32),
-        pltpu.VMEM((depth * 2, 8, tok), f32),
-        dma(()), dma((loads,)), dma((depth * 2,)), dma((depth * 2,)),
+        pltpu.VMEM((experts, 8, 2 * capacity), f32), pltpu.VMEM((128, tok), f32),
+        pltpu.VMEM((depth * 2, top, tok), jnp.int32), pltpu.VMEM((depth * 2, top, tok), f32),
+        dma((3,)), dma((3, experts)), dma((2, depth * 2)), dma((2, depth * 2)),
         dma((depth, 2)), dma((depth, 2)), dma((depth, 6)), dma((depth, 6)),
         dma((depth, 8)), dma((depth, 8)), dma((depth, 4)), dma((depth, 4)),
         dma((depth, 6)), dma((depth, 6)), dma((depth,)), dma((depth,)),
     ]
-    return pl.pallas_call(
+    mixed = pl.pallas_call(
         fused_kernel,
-        out_shape=jax.ShapeDtypeStruct((tok, feat), bf16),
-        in_specs=[any_space, vmem, any_space, any_space, any_space],
-        out_specs=vmem,
+        out_shape=jax.ShapeDtypeStruct((feat, tok), bf16),
+        in_specs=[pl.BlockSpec(memory_space=pl.ANY)] * 6,
+        out_specs=pl.BlockSpec(memory_space=pltpu.VMEM),
         scratch_shapes=scratch,
         compiler_params=pltpu.CompilerParams(
             collective_id=0, has_side_effects=True, vmem_limit_bytes=63 * 1024 * 1024),
-    )(tokens, meta, gate_weight, up_weight, down_weight)
+    )(tokens.T, expert_ids.T, combine_weights.T, gate_weight.transpose(0, 2, 1),
+      up_weight.transpose(0, 2, 1), down_weight)
+    return mixed.T
 
 
 def local(tokens, expert_ids, combine_weights, gate_weight, up_weight, down_weight):

time: 159 us -> 124 us (0.78)
  the two profiles are of different devices: /device:TPU:12 before, /device:TPU:8 now
where the time goes in v2:
time: 124 us
  Pallas kernels  122 us (98%)
  local copies, waits for them, and re-layouts  1.75 us (1%)
    pallas_call x1, Pallas kernels, fused(): pl.pallas_call(fused_kernel, out_shape=jax.ShapeDtypeStruct((feat, tok),...  122 us

profile of v2, /device:TPU:8, one launch (start us, length us, event | category | flops | bytes accessed | tf_op | source)
XLA Modules:
  0.0 123.6 jit_solution(5673806104865506402)
XLA Ops:
  0.0 121.8 %shard_map.64 = bf16[720,256]{1,0:T(8,128)(2,1)} custom-call(bf16[720,256]{1,0:T(8,128)(2,1)} %bitcast.9, s32[4,256]{1,0:T(4,128)} %bitcast.10, f32[4,256]{1,0:T(4,128)} %bitcast.11, bf16[2,720,2880]{2,1,0:T(8,128)(2,1)} %bitcast.6, bf16[2,720,2880]{2,1,0:T(8,128)(2,1)} %bitcast.7, bf16[2,720,2880]{2,1,0:T(8,128)(2,1)} %down.1), custom_call_target="tpu_custom_call" | custom-call | tf_op jit(solution)/shard_map/pallas_call | solution.py:650
  121.8 1.7 %copy.8 = bf16[256,720]{0,1:T(8,128)(2,1)} copy(bf16[256,720]{0,1:T(8,128)(2,1)} %bitcast.8) | data formatting | bytes 737280

commit v3 on v2

--- a/solution.py
+++ b/solution.py
@@ -263,6 +263,14 @@
 
 
 STEP = 240
+def when(condition, run):
+    if isinstance(condition, bool):
+        if condition:
+            run()
+    else:
+        pl.when(condition)(run)
+
+
 PUSHES = (((0, 0), 0, "x"), ((0, 0), 1, "y"), ((0, 0), 0, "y"), ((0, 0), 1, "x"),
           ((1, 0), 0, "y"), ((0, 1), 1, "x"))
 
@@ -272,16 +280,24 @@
         e, t = lax.axis_index("ep"), lax.axis_index("tp")
         self.ep, self.tp = e, t
         self.z, self.x, self.y, self.c = e // 2, e % 2, t // 2, t % 2
+        self.mid = (self.z + 1) // 2 % 2
+
+    def away(self, m, dx=0, dy=0, dc=0):
+        z = (self.z // 2 + m // 2) % 2 * 2 + (self.z % 2 + m % 2) % 2
+        return z * 2 + (self.x + dx) % 2, (self.y + dy) % 2 * 2 + (self.c + dc) % 2
 
     def device(self, k=0, dx=0, dy=0, dc=0):
-        z = (self.z // 2 + k // 2) % 2 * 2 + (self.z % 2 + k % 2) % 2
-        return z * 2 + (self.x + dx) % 2, (self.y + dy) % 2 * 2 + (self.c + dc) % 2
+        return self.away((k + self.mid * (4 - 2 * k)) % 4, dx, dy, dc)
+
+    def seen(self, k):
+        return 3 - 2 * self.mid if k % 2 else k
 
 
 def fused_kernel(tokens, ids, scales, gate, up, down, out, buf, inc, from_y, from_x, last_x, last_y,
-                 from_z, wide, deep, stage, rows, hid, take, back, weigh, place, all_ids, all_scales,
+                 from_z, aside, wide, deep, stage, rows, hid, take, back, weigh, place, all_ids, all_scales,
                  own_sem, w_sem, meta_send, meta_recv, z_send, z_recv, lane_send, lane_recv,
-                 pair_send, pair_recv, sp_send, sp_recv, sx_send, sx_recv, sz_send, sz_recv):
+                 pair_send, pair_recv, sp_send, sp_recv, sx_send, sx_recv, sz_send, sz_recv,
+                 cross_send, cross_recv, ferry_send, ferry_recv):
     f32, bf16 = jnp.float32, jnp.bfloat16
     here = Grid()
     depth = from_z.shape[0] + 1
@@ -302,9 +318,27 @@
             src_ref=src, dst_ref=dst, send_sem=send, recv_sem=recv,
             device_id=to, device_id_type=MESH)
 
-    def z_push(k, p):
-        return remote(tokens.at[parts[p]], buf.at[cell(k, 0, 0, 0), parts[p]],
-                      z_send.at[k, p], z_recv.at[k, p], here.device(k=k))
+    near, other = here.away(1), here.away(3)
+    mid, end = here.mid == 1, here.mid == 0
+
+    def flow(n, p):
+        source, label = ((None, here.seen(1)), (None, 1), (1, 2), (3, 2), (2, 3))[n]
+        src = tokens if source is None else buf.at[cell(source, 0, 0, 0)]
+        return remote(src.at[parts[p]], buf.at[cell(label, 0, 0, 0), parts[p]],
+                      z_send.at[n, p], z_recv.at[label, p], other if n in (1, 3) else near)
+
+    def flow_start(n):
+        flow(n, 0).start()
+        flow(n, 1).start()
+
+    def flow_sent(n):
+        flow(n, 0).wait_send()
+        flow(n, 1).wait_send()
+
+    def arrive(k):
+        for p in (0, 1):
+            at = buf.at[cell(k, 0, 0, 0), parts[p]]
+            remote(at, at, z_send.at[0, p], z_recv.at[k, p], near).wait_recv()
 
     def lane_push(k, n):
         (dx, dy), p, axis = PUSHES[n]
@@ -333,8 +367,9 @@
             for copy in self.copies:
                 copy.wait_send()
 
-    def meta_push(k, dx):
-        n, to = k * 2 + dx, here.device(k=k, dx=dx)
+    def meta_push(k, dx, to_me=False):
+        to = here.device(k=k, dx=dx)
+        n = k * 2 + dx if to_me else here.seen(k) * 2 + dx
         return Both(remote(ids, all_ids.at[n], meta_send.at[0, n], meta_recv.at[0, n], to),
                     remote(scales, all_scales.at[n], meta_send.at[1, n], meta_recv.at[1, n], to))
 
@@ -345,16 +380,43 @@
         pair(k, 0, 0, 1).start()
 
     def column(k):
-        z_push(k, 0).wait_recv()
-        z_push(k, 1).wait_recv()
+        if k == 3:
+            when(end, lambda: arrive(3))
+        else:
+            arrive(k)
+            when(mid, lambda: flow_start(2 if k == 1 else 4))
         gather_a(k)
+
+    def turn_early():
+        arrive(3)
+        flow_start(3)
+
+    def cross(n, p):
+        source, label = ((0, 3), (2, 3), (1, 2))[n]
+        return remote(buf.at[cell(source, 1, 1, 0), parts[p]],
+                      buf.at[cell(label, 1, 1, 0), parts[p]],
+                      cross_send.at[n, p], cross_recv.at[label - 2, p], near)
+
+    def crossed(k, p):
+        at = buf.at[cell(k, 1, 1, 0), parts[p]]
+        remote(at, at, cross_send.at[0, p], cross_recv.at[k - 2, p], near).wait_recv()
+
+    def inside(k):
+        if isinstance(k, int):
+            return (True, True, mid, False)[k]
+        return k < 2 + here.mid
+
+    def outside(k):
+        if isinstance(k, int):
+            return (False, False, end, True)[k]
+        return k >= 2 + here.mid
 
     def gather_b(k):
         lane_push(k, 0).wait_recv()
-        lane_push(k, 4).start()
+        when(inside(k), lambda: lane_push(k, 4).start())
         pair(k, 1, 0, 0).start()
         lane_push(k, 1).wait_recv()
-        lane_push(k, 5).start()
+        when(inside(k), lambda: lane_push(k, 5).start())
         pair(k, 0, 1, 1).start()
 
     def gather_c(k, first):
@@ -364,10 +426,19 @@
             lane_push(k, 3).wait_recv()
             pair(k, 1, 0, 1).start()
         else:
-            lane_push(k, 4).wait_recv()
-            pair(k, 1, 1, 0).start()
-            lane_push(k, 5).wait_recv()
-            pair(k, 1, 1, 1).start()
+            for p in (0, 1):
+                def relayed():
+                    lane_push(k, 4 + p).wait_recv()
+                    if isinstance(k, int):
+                        if k == 0:
+                            when(end, lambda: cross(0, p).start())
+                        if k == 1:
+                            when(mid, lambda: cross(2, p).start())
+                    else:
+                        when((k == 2) & mid, lambda: cross(1, p).start())
+                when(inside(k), relayed)
+                when(outside(k), lambda: crossed(k, p))
+                pair(k, 1, 1, p).start()
 
     def gather_d(k):
         for dx in (0, 1):
@@ -376,8 +447,26 @@
                     pair(k, dx, dy, p).wait_recv()
 
     def gather_sent(k):
-        for n in range(6):
+        for n in range(4):
             lane_push(k, n).wait_send()
+
+        def relayed():
+            for p in (0, 1):
+                lane_push(k, 4 + p).wait_send()
+        when(inside(k), relayed)
+        for at, n, side in ((0, 0, end), (2, 1, mid), (1, 2, mid)):
+            @pl.when((k == at) & side)
+            def _():
+                cross(n, 0).wait_send()
+                cross(n, 1).wait_send()
+
+        @pl.when(mid)
+        def _():
+            for at, n in ((1, 2), (3, 3), (2, 4)):
+                @pl.when(k == at)
+                def _():
+                    flow_sent(n)
+
         for dx in (0, 1):
             for dy in (0, 1):
                 for p in (0, 1):
@@ -398,39 +487,79 @@
             (buf.at[cell(k, 0, 1, 0), high], last_y.at[k], "y"))[n]
         return remote(src, dst, sx_send.at[k, n], sx_recv.at[k, n], over[axis])
 
-    def home(k):
-        return remote(buf.at[cell(k, 0, 0, 0)], from_z.at[k - 1],
-                      sz_send.at[k], sz_recv.at[k], here.device(k=k))
+    def home(k, to_me=False):
+        at = k if to_me else here.seen(k)
+        return remote(buf.at[cell(k, 0, 0, 0)], from_z.at[at - 1],
+                      sz_send.at[k], sz_recv.at[at], here.device(k=k))
 
     def add(at, part, got):
         buf[at, part] = (buf[at, part].astype(f32) + got.astype(f32)).astype(bf16)
 
-    def scatter_b(k):
-        for dx, dy in ((1, 1), (0, 1), (1, 0), (0, 0)):
-            give(k, dx, dy).wait_recv()
-            add(cell(k, dx, dy, 0), pl.ds(0, feat), inc[k * 4 + dx * 2 + dy])
-            if dy:
-                hop(k, 1 - dx).start()
-            if dx:
-                hop(k, 3 - dy).start()
-
-    def scatter_c(k):
+    def ferry(k):
+        slot = 1 - here.mid if k == 1 else k - 2
+        return remote(buf.at[cell(k, 1, 1, 0)], aside.at[slot], ferry_send.at[k - 1],
+                      ferry_recv.at[slot], here.away(1 + 2 * here.mid) if k == 1 else near)
+
+    def ferried(k, slot):
+        remote(aside.at[slot], aside.at[slot], ferry_send.at[0], ferry_recv.at[slot],
+               near).wait_recv()
+        add(cell(k, 1, 1, 0), pl.ds(0, feat), aside[slot])
+
+    def merge(k, dx, dy):
+        give(k, dx, dy).wait_recv()
+        add(cell(k, dx, dy, 0), pl.ds(0, feat), inc[k * 4 + dx * 2 + dy])
+
+    def scatter_near(k):
+        merge(k, 1, 1)
+        ferry(k).start()
+        merge(k, 0, 1)
+        hop(k, 1).start()
+        hop(k, 5).start()
+        merge(k, 1, 0)
+        hop(k, 3).start()
+        hop(k, 4).start()
+        merge(k, 0, 0)
+
+    def scatter_sides(k):
+        merge(k, 0, 1)
+        hop(k, 1).start()
+        merge(k, 1, 0)
+        hop(k, 3).start()
+        merge(k, 0, 0)
+
+    def scatter_corner(k):
+        merge(k, 1, 1)
+        if k == 0:
+            when(mid, lambda: ferried(0, 0))
+            when(mid, lambda: ferried(0, 1))
+        if k == 3:
+            when(end, lambda: ferried(3, 0))
+        hop(k, 0).start()
+        hop(k, 2).start()
+
+    def scatter_far(k):
+        scatter_corner(k)
+        scatter_sides(k)
+
+    def scatter_turn(k):
         hop(k, 0).wait_recv()
         add(cell(k, 1, 0, 0), low, from_y[k * 2 + 1])
         hop(k, 4).start()
         hop(k, 2).wait_recv()
         add(cell(k, 0, 1, 0), high, from_x[k * 2 + 1])
         hop(k, 5).start()
+
+    def scatter_end(k):
         hop(k, 1).wait_recv()
         add(cell(k, 0, 0, 0), low, from_y[k * 2])
         hop(k, 3).wait_recv()
         add(cell(k, 0, 0, 0), high, from_x[k * 2])
-
-    def scatter_d(k):
         hop(k, 4).wait_recv()
         add(cell(k, 0, 0, 0), low, last_x[k])
         hop(k, 5).wait_recv()
         add(cell(k, 0, 0, 0), high, last_y[k])
+        if k:
+            home(k).start()
 
     own = [pltpu.make_async_copy(tokens, buf.at[cell(0, 0, 0, 0)], own_sem.at[0]),
            pltpu.make_async_copy(ids, all_ids.at[0], own_sem.at[1]),
@@ -438,18 +567,17 @@
     for copy in own:
         copy.start()
     barrier = pltpu.get_barrier_semaphore()
-    near = [here.device(k=k, dx=dx) for k in range(depth) for dx in (0, 1) if k or dx]
-    near += [over["y"], partner]
-    for who in near:
+    greeted = [here.device(k=k, dx=dx) for k in range(depth) for dx in (0, 1) if k or dx]
+    greeted += [over["y"], partner]
+    for who in greeted:
         pl.semaphore_signal(barrier, inc=1, device_id=who, device_id_type=MESH)
-    pl.semaphore_wait(barrier, len(near))
+    pl.semaphore_wait(barrier, len(greeted))
     for k in range(depth):
         for dx in (0, 1):
             if k or dx:
                 meta_push(k, dx).start()
-    for k in range(1, depth):
-        z_push(k, 0).start()
-        z_push(k, 1).start()
+    flow_start(0)
+    when(mid, lambda: flow_start(1))
     for copy in own:
         copy.wait()
     gather_a(0)
@@ -475,14 +603,8 @@
 
     turn(0)
     gather_b(0)
+    when(mid, turn_early)
     column(1)
-    for e in range(1, experts):
-        turn(e)
-    gather_c(0, True)
-    gather_c(0, False)
-    for load in loads:
-        load.wait()
-
     ahead = (lax.broadcasted_iota(jnp.int32, (tok, tok), 0)
              < lax.broadcasted_iota(jnp.int32, (tok, tok), 1)).astype(f32).astype(bf16)
     slot_row = lax.broadcasted_iota(jnp.int32, (cap, tok), 0).astype(f32)
@@ -509,12 +631,28 @@
             for e in range(experts):
                 n = dx * experts + e
                 at = pl.ds(e * cap, cap)
-                take[dx, at, :] = (slot_row == slot[n:n + 1, :]).astype(f32).astype(bf16)
+                take[k, dx, at, :] = (slot_row == slot[n:n + 1, :]).astype(f32).astype(bf16)
                 hot = (slot_col == turned[:, n:n + 1]).astype(f32)
-                back[dx, :, at] = hot.astype(bf16)
+                back[k, dx, :, at] = hot.astype(bf16)
                 held = turned[:, 2 * experts + n:2 * experts + n + 1]
-                weigh[e, :, pl.ds(dx * cap, cap)] = jnp.broadcast_to(
+                weigh[k, e, :, pl.ds(dx * cap, cap)] = jnp.broadcast_to(
                     jnp.sum(hot * held, axis=0, keepdims=True), (8, cap))
+
+    def prepare(k, carry):
+        @pl.when(k > 0)
+        def _():
+            meta_push(k, 0, True).wait_recv()
+        meta_push(k, 1, True).wait_recv()
+        masks(k)
+        return carry
+
+    for e in range(1, experts):
+        turn(e)
+    lax.fori_loop(0, depth, prepare, 0)
+    gather_c(0, True)
+    gather_c(0, False)
+    for load in loads:
+        load.wait()
 
     def block(k, dx, j):
         return cell(k, dx, (here.y + j // 2) % 2, (here.c + j % 2) % 2)
@@ -522,17 +660,17 @@
     def dispatch(k):
         for dx in (0, 1):
             for j in range(4):
-                got = jnp.dot(buf[block(k, dx, j)], back[dx], preferred_element_type=f32)
+                got = jnp.dot(buf[block(k, dx, j)], back[k, dx], preferred_element_type=f32)
                 rows[dx, pl.ds(j * feat, feat), :] = got.astype(bf16)
 
-    def enter(e):
+    def enter(k, e):
         at = pl.ds(e * cap, cap)
         held = jnp.concatenate([rows[0, :, at], rows[1, :, at]], axis=1)
         for n in range(0, ff, STEP):
             part = pl.ds(n, min(STEP, ff - n))
             g = jnp.dot(wide[0, e, part, :], held, preferred_element_type=f32)
             u = jnp.dot(wide[1, e, part, :], held, preferred_element_type=f32)
-            hid[part, :] = act_weighted(g, u, weigh[e, 0:1, :])
+            hid[part, :] = act_weighted(g, u, weigh[k, e, 0:1, :])
 
     def leave(e):
         at = pl.ds(e * cap, cap)
@@ -544,42 +682,80 @@
 
     def combine(k, dx):
         for j in range(4):
-            got = jnp.dot(rows[dx, pl.ds(j * feat, feat), :], take[dx], preferred_element_type=f32)
+            got = jnp.dot(rows[dx, pl.ds(j * feat, feat), :], take[k, dx], preferred_element_type=f32)
             buf[block(k, dx, j)] = got.astype(bf16)
 
-    def plane(k, carry):
+    def at(condition):
+        return pl.when(condition)
+
+    def plane(step, carry):
         last = depth - 1
+        k = (step + here.mid) % depth
+        ahead_of = (k < last) & (end | (k > 0))
         gather_d(k)
-
-        @pl.when(k > 0)
-        def _():
-            meta_push(k, 0).wait_recv()
-        meta_push(k, 1).wait_recv()
-        masks(k)
         dispatch(k)
 
-        @pl.when(k < last)
-        def _():
-            gather_b(k + 1)
-        enter(0)
-
-        @pl.when(k < last - 1)
-        def _():
-            column(k + 2)
-
-        @pl.when(k > 1)
-        def _():
-            scatter_b(k - 1)
+        @at((k == 0) & mid)
+        def _():
+            scatter_far(3)
+            scatter_end(2)
+
+        @at((k == 2) & end)
+        def _():
+            scatter_near(1)
+            scatter_sides(0)
+
+        @at((k == last) & end)
+        def _():
+            scatter_far(2)
+        enter(k, 0)
+
+        @at((k == 0) & end)
+        def _():
+            gather_b(1)
+
+        @at(k == 1)
+        def _():
+            gather_b(2)
+            column(3)
+
+        @at((k == 2) & mid)
+        def _():
+            scatter_near(1)
+
+        @at((k == last) & mid)
+        def _():
+            scatter_near(2)
         leave(0)
-        enter(1)
-
-        @pl.when(k < last)
+
+        @at((k == 0) & end)
+        def _():
+            column(2)
+
+        @at((k == 0) & mid)
+        def _():
+            scatter_turn(3)
+        enter(k, 1)
+
+        @at(k == 2)
+        def _():
+            gather_b(3)
+
+        @at(ahead_of)
         def _():
             gather_c(k + 1, True)
+
+        @at(k == last)
+        def _():
+            scatter_end(1)
         leave(1)
+
+        @at((k == last) & end)
+        def _():
+            scatter_turn(2)
         gather_sent(k)
 
-        @pl.when(k < last)
+        @at(ahead_of)
         def _():
             gather_c(k + 1, False)
         for dx in (1, 0):
@@ -588,24 +764,30 @@
             give(k, dx, 0).start()
         return carry
 
+    @pl.when(mid)
+    def _():
+        gather_b(1)
+        column(2)
+        gather_c(1, True)
+        gather_c(1, False)
     lax.fori_loop(0, depth, plane, 0)
 
-    scatter_c(1)
-    scatter_b(3)
-    scatter_c(2)
-    scatter_d(1)
-    home(1).start()
-    scatter_b(0)
-    scatter_c(3)
-    scatter_d(2)
-    home(2).start()
-    scatter_c(0)
-    scatter_d(3)
-    home(3).start()
-    scatter_d(0)
+    @pl.when(end)
+    def _():
+        scatter_far(3)
+        scatter_end(2)
+        scatter_turn(3)
+        scatter_corner(0)
+
+    @pl.when(mid)
+    def _():
+        scatter_far(0)
+    scatter_end(3)
+    scatter_turn(0)
+    scatter_end(0)
     total = buf[cell(0, 0, 0, 0)].astype(f32)
     for k in range(1, depth):
-        home(k).wait_recv()
+        home(k, True).wait_recv()
         total = total + from_z[k - 1].astype(f32)
     out[...] = total.astype(out.dtype)
     for k in range(depth):
@@ -614,12 +796,25 @@
                 meta_push(k, dx).wait_send()
             for dy in (0, 1):
                 give(k, dx, dy).wait_send()
-        for n in range(6):
+        for n in (1, 3, 4, 5):
             hop(k, n).wait_send()
+
+        def cornered():
+            hop(k, 0).wait_send()
+            hop(k, 2).wait_send()
+        if k == 2:
+            when(end, cornered)
+        elif k != 1:
+            cornered()
         if k:
-            z_push(k, 0).wait_send()
-            z_push(k, 1).wait_send()
             home(k).wait_send()
+    ferry(1).wait_send()
+    flow_sent(0)
+
+    @pl.when(mid)
+    def _():
+        ferry(2).wait_send()
+        flow_sent(1)
 
 
 def fused(tokens, expert_ids, combine_weights, gate_weight, up_weight, down_weight, depth, capacity):
@@ -634,18 +829,20 @@
         pltpu.VMEM((depth * 8, feat, tok), bf16), pltpu.VMEM((depth * 4, feat, tok), bf16),
         pltpu.VMEM((depth * 2, half, tok), bf16), pltpu.VMEM((depth * 2, rest, tok), bf16),
         pltpu.VMEM((depth, half, tok), bf16), pltpu.VMEM((depth, rest, tok), bf16),
-        pltpu.VMEM((depth - 1, feat, tok), bf16),
+        pltpu.VMEM((depth - 1, feat, tok), bf16), pltpu.VMEM((2, feat, tok), bf16),
         pltpu.VMEM((2, experts, ff, width), bf16), pltpu.VMEM((experts, width, ff), bf16),
         pltpu.VMEM((ff, width), bf16),
         pltpu.VMEM((2, width, experts * capacity), bf16),
         pltpu.VMEM((ff, 2 * capacity), bf16),
-        pltpu.VMEM((2, experts * capacity, tok), bf16), pltpu.VMEM((2, tok, experts * capacity), bf16),
-        pltpu.VMEM((experts, 8, 2 * capacity), f32), pltpu.VMEM((128, tok), f32),
+        pltpu.VMEM((depth, 2, experts * capacity, tok), bf16),
+        pltpu.VMEM((depth, 2, tok, experts * capacity), bf16),
+        pltpu.VMEM((depth, experts, 8, 2 * capacity), f32), pltpu.VMEM((128, tok), f32),
         pltpu.VMEM((depth * 2, top, tok), jnp.int32), pltpu.VMEM((depth * 2, top, tok), f32),
         dma((3,)), dma((3, experts)), dma((2, depth * 2)), dma((2, depth * 2)),
-        dma((depth, 2)), dma((depth, 2)), dma((depth, 6)), dma((depth, 6)),
+        dma((5, 2)), dma((depth, 2)), dma((depth, 6)), dma((depth, 6)),
         dma((depth, 8)), dma((depth, 8)), dma((depth, 4)), dma((depth, 4)),
         dma((depth, 6)), dma((depth, 6)), dma((depth,)), dma((depth,)),
+        dma((3, 2)), dma((2, 2)), dma((2,)), dma((2,)),
     ]
     mixed = pl.pallas_call(
         fused_kernel,

time: 124 us -> 110 us (0.89)
  the two profiles are of different devices: /device:TPU:8 before, /device:TPU:0 now
where the time goes in v3:
time: 110 us
  Pallas kernels  108 us (98%)
  local copies, waits for them, and re-layouts  1.75 us (2%)
    pallas_call x1, Pallas kernels, fused(): pl.pallas_call(fused_kernel, out_shape=jax.ShapeDtypeStruct((feat, tok),...  108 us

profile of v3, /device:TPU:0, one launch (start us, length us, event | category | flops | bytes accessed | tf_op | source)
XLA Modules:
  0.0 110.0 jit_solution(18382340822622554184)
XLA Ops:
  0.0 108.2 %shard_map.64 = bf16[720,256]{1,0:T(8,128)(2,1)} custom-call(bf16[720,256]{1,0:T(8,128)(2,1)} %bitcast.9, s32[4,256]{1,0:T(4,128)} %bitcast.10, f32[4,256]{1,0:T(4,128)} %bitcast.11, bf16[2,720,2880]{2,1,0:T(8,128)(2,1)} %bitcast.6, bf16[2,720,2880]{2,1,0:T(8,128)(2,1)} %bitcast.7, bf16[2,720,2880]{2,1,0:T(8,128)(2,1)} %down.1), custom_call_target="tpu_custom_call" | custom-call | tf_op jit(solution)/shard_map/pallas_call | solution.py:847
  108.2 1.7 %copy.8 = bf16[256,720]{0,1:T(8,128)(2,1)} copy(bf16[256,720]{0,1:T(8,128)(2,1)} %bitcast.8) | data formatting | bytes 737280

commit v4 on v3

--- a/solution.py
+++ b/solution.py
@@ -294,10 +294,10 @@
 
 
 def fused_kernel(tokens, ids, scales, gate, up, down, out, buf, inc, from_y, from_x, last_x, last_y,
-                 from_z, aside, wide, deep, stage, rows, hid, take, back, weigh, place, all_ids, all_scales,
+                 from_z, aside, passing, wide, deep, stage, rows, hid, take, back, weigh, place, all_ids, all_scales,
                  own_sem, w_sem, meta_send, meta_recv, z_send, z_recv, lane_send, lane_recv,
                  pair_send, pair_recv, sp_send, sp_recv, sx_send, sx_recv, sz_send, sz_recv,
-                 cross_send, cross_recv, ferry_send, ferry_recv):
+                 cross_send, cross_recv, ferry_send, ferry_recv, detour_sem):
     f32, bf16 = jnp.float32, jnp.bfloat16
     here = Grid()
     depth = from_z.shape[0] + 1
@@ -487,10 +487,19 @@
             (buf.at[cell(k, 0, 1, 0), high], last_y.at[k], "y"))[n]
         return remote(src, dst, sx_send.at[k, n], sx_recv.at[k, n], over[axis])
 
-    def home(k, to_me=False):
+    def home(k, p, to_me=False):
         at = k if to_me else here.seen(k)
-        return remote(buf.at[cell(k, 0, 0, 0)], from_z.at[at - 1],
-                      sz_send.at[k], sz_recv.at[at], here.device(k=k))
+        return remote(buf.at[cell(k, 0, 0, 0), parts[p]], from_z.at[at - 1, parts[p]],
+                      sz_send.at[k, p], sz_recv.at[at, p], here.device(k=k))
+
+    def detour():
+        return remote(buf.at[cell(3, 0, 0, 0), high], passing,
+                      detour_sem.at[0], detour_sem.at[1], here.device(k=2))
+
+    def onward():
+        detour().wait_recv()
+        add(cell(3, 0, 0, 0), high, passing[...])
+        home(3, 1).start()
 
     def add(at, part, got):
         buf[at, part] = (buf[at, part].astype(f32) + got.astype(f32)).astype(bf16)
@@ -509,9 +518,13 @@
         give(k, dx, dy).wait_recv()
         add(cell(k, dx, dy, 0), pl.ds(0, feat), inc[k * 4 + dx * 2 + dy])
 
-    def scatter_near(k):
+    def scatter_ferry(k):
         merge(k, 1, 1)
         ferry(k).start()
+
+    def scatter_near(k):
+        if k == 1:
+            scatter_ferry(k)
         merge(k, 0, 1)
         hop(k, 1).start()
         hop(k, 5).start()
@@ -558,8 +571,12 @@
         add(cell(k, 0, 0, 0), low, last_x[k])
         hop(k, 5).wait_recv()
         add(cell(k, 0, 0, 0), high, last_y[k])
-        if k:
-            home(k).start()
+        if k == 3:
+            when(end, lambda: detour().start())
+            home(3, 0).start()
+        elif k:
+            home(k, 0).start()
+            home(k, 1).start()
 
     own = [pltpu.make_async_copy(tokens, buf.at[cell(0, 0, 0, 0)], own_sem.at[0]),
            pltpu.make_async_copy(ids, all_ids.at[0], own_sem.at[1]),
@@ -700,14 +717,10 @@
             scatter_far(3)
             scatter_end(2)
 
-        @at((k == 2) & end)
-        def _():
-            scatter_near(1)
-            scatter_sides(0)
-
-        @at((k == last) & end)
-        def _():
-            scatter_far(2)
+        @at(k == last)
+        def _():
+            when(mid, lambda: scatter_ferry(2))
+            when(end, lambda: scatter_far(2))
         enter(k, 0)
 
         @at((k == 0) & end)
@@ -719,13 +732,14 @@
             gather_b(2)
             column(3)
 
-        @at((k == 2) & mid)
+        @at(k == 2)
         def _():
             scatter_near(1)
 
-        @at((k == last) & mid)
-        def _():
-            scatter_near(2)
+        @at(k == last)
+        def _():
+            when(mid, lambda: scatter_near(2))
+            scatter_end(1)
         leave(0)
 
         @at((k == 0) & end)
@@ -745,9 +759,6 @@
         def _():
             gather_c(k + 1, True)
 
-        @at(k == last)
-        def _():
-            scatter_end(1)
         leave(1)
 
         @at((k == last) & end)
@@ -777,19 +788,26 @@
         scatter_far(3)
         scatter_end(2)
         scatter_turn(3)
-        scatter_corner(0)
-
-    @pl.when(mid)
-    def _():
-        scatter_far(0)
+
+    scatter_far(0)
     scatter_end(3)
     scatter_turn(0)
+    when(mid, onward)
     scatter_end(0)
-    total = buf[cell(0, 0, 0, 0)].astype(f32)
-    for k in range(1, depth):
-        home(k, True).wait_recv()
-        total = total + from_z[k - 1].astype(f32)
-    out[...] = total.astype(out.dtype)
+    for p in (0, 1):
+        total = buf[cell(0, 0, 0, 0), parts[p]].astype(f32)
+        for k in range(1, depth - p):
+            home(k, p, True).wait_recv()
+            total = total + from_z[k - 1, parts[p]].astype(f32)
+        if p == 0:
+            out[low, :] = total.astype(out.dtype)
+        else:
+            when(end, lambda: out.__setitem__((high, slice(None)), total.astype(out.dtype)))
+
+            @pl.when(mid)
+            def _():
+                home(3, 1, True).wait_recv()
+                out[high, :] = (total + from_z[2, high].astype(f32)).astype(out.dtype)
     for k in range(depth):
         for dx in (0, 1):
             if k or dx:
@@ -807,7 +825,10 @@
         elif k != 1:
             cornered()
         if k:
-            home(k).wait_send()
+            home(k, 0).wait_send()
+        if k in (1, 2):
+            home(k, 1).wait_send()
+    when(end, lambda: detour().wait_send())
     ferry(1).wait_send()
     flow_sent(0)
 
@@ -815,6 +836,7 @@
     def _():
         ferry(2).wait_send()
         flow_sent(1)
+        home(3, 1).wait_send()
 
 
 def fused(tokens, expert_ids, combine_weights, gate_weight, up_weight, down_weight, depth, capacity):
@@ -830,6 +852,7 @@
         pltpu.VMEM((depth * 2, half, tok), bf16), pltpu.VMEM((depth * 2, rest, tok), bf16),
         pltpu.VMEM((depth, half, tok), bf16), pltpu.VMEM((depth, rest, tok), bf16),
         pltpu.VMEM((depth - 1, feat, tok), bf16), pltpu.VMEM((2, feat, tok), bf16),
+        pltpu.VMEM((rest, tok), bf16),
         pltpu.VMEM((2, experts, ff, width), bf16), pltpu.VMEM((experts, width, ff), bf16),
         pltpu.VMEM((ff, width), bf16),
         pltpu.VMEM((2, width, experts * capacity), bf16),
@@ -841,8 +864,8 @@
         dma((3,)), dma((3, experts)), dma((2, depth * 2)), dma((2, depth * 2)),
         dma((5, 2)), dma((depth, 2)), dma((depth, 6)), dma((depth, 6)),
         dma((depth, 8)), dma((depth, 8)), dma((depth, 4)), dma((depth, 4)),
-        dma((depth, 6)), dma((depth, 6)), dma((depth,)), dma((depth,)),
-        dma((3, 2)), dma((2, 2)), dma((2,)), dma((2,)),
+        dma((depth, 6)), dma((depth, 6)), dma((depth, 2)), dma((depth, 2)),
+        dma((3, 2)), dma((2, 2)), dma((2,)), dma((2,)), dma((2,)),
     ]
     mixed = pl.pallas_call(
         fused_kernel,

time: 110 us -> 104 us (0.945)
  Pallas kernels: 108 us -> 102 us
    pallas_call x1, Pallas kernels: 108 us -> 102 us  [fused(): pl.pallas_call(fused_kernel, out_shape=jax.ShapeDtypeStruct((feat, tok),...]
where the time goes in v4:
time: 104 us
  Pallas kernels  102 us (98%)
  local copies, waits for them, and re-layouts  1.75 us (2%)
    pallas_call x1, Pallas kernels, fused(): pl.pallas_call(fused_kernel, out_shape=jax.ShapeDtypeStruct((feat, tok),...  102 us

profile of v4, /device:TPU:0, one launch (start us, length us, event | category | flops | bytes accessed | tf_op | source)
XLA Modules:
  0.0 103.8 jit_solution(15732269829700980135)
XLA Ops:
  0.0 102.1 %shard_map.64 = bf16[720,256]{1,0:T(8,128)(2,1)} custom-call(bf16[720,256]{1,0:T(8,128)(2,1)} %bitcast.9, s32[4,256]{1,0:T(4,128)} %bitcast.10, f32[4,256]{1,0:T(4,128)} %bitcast.11, bf16[2,720,2880]{2,1,0:T(8,128)(2,1)} %bitcast.6, bf16[2,720,2880]{2,1,0:T(8,128)(2,1)} %bitcast.7, bf16[2,720,2880]{2,1,0:T(8,128)(2,1)} %down.1), custom_call_target="tpu_custom_call" | custom-call | tf_op jit(solution)/shard_map/pallas_call | solution.py:870
  102.1 1.7 %copy.8 = bf16[256,720]{0,1:T(8,128)(2,1)} copy(bf16[256,720]{0,1:T(8,128)(2,1)} %bitcast.8) | data formatting | bytes 737280

commit v5 on v4

--- a/solution.py
+++ b/solution.py
@@ -505,8 +505,8 @@
         buf[at, part] = (buf[at, part].astype(f32) + got.astype(f32)).astype(bf16)
 
     def ferry(k):
-        slot = 1 - here.mid if k == 1 else k - 2
-        return remote(buf.at[cell(k, 1, 1, 0)], aside.at[slot], ferry_send.at[k - 1],
+        slot = (2, 1 - here.mid, 0)[k]
+        return remote(buf.at[cell(k, 1, 1, 0)], aside.at[slot], ferry_send.at[k],
                       ferry_recv.at[slot], here.away(1 + 2 * here.mid) if k == 1 else near)
 
     def ferried(k, slot):
@@ -547,6 +547,7 @@
             when(mid, lambda: ferried(0, 1))
         if k == 3:
             when(end, lambda: ferried(3, 0))
+            when(mid, lambda: ferried(3, 2))
         hop(k, 0).start()
         hop(k, 2).start()
 
@@ -574,6 +575,10 @@
         if k == 3:
             when(end, lambda: detour().start())
             home(3, 0).start()
+            when(end, lambda: home(2, 1).start())
+        elif k == 2:
+            home(2, 0).start()
+            when(mid, lambda: home(2, 1).start())
         elif k:
             home(k, 0).start()
             home(k, 1).start()
@@ -735,6 +740,7 @@
         @at(k == 2)
         def _():
             scatter_near(1)
+            when(end, lambda: scatter_ferry(0))
 
         @at(k == last)
         def _():
@@ -759,11 +765,12 @@
         def _():
             gather_c(k + 1, True)
 
+        @at((k == last) & end)
+        def _():
+            scatter_turn(2)
+
         leave(1)
 
-        @at((k == last) & end)
-        def _():
-            scatter_turn(2)
         gather_sent(k)
 
         @at(ahead_of)
@@ -788,11 +795,15 @@
         scatter_far(3)
         scatter_end(2)
         scatter_turn(3)
-
-    scatter_far(0)
-    scatter_end(3)
-    scatter_turn(0)
-    when(mid, onward)
+        scatter_near(0)
+        scatter_end(3)
+
+    @pl.when(mid)
+    def _():
+        scatter_far(0)
+        scatter_end(3)
+        scatter_turn(0)
+        onward()
     scatter_end(0)
     for p in (0, 1):
         total = buf[cell(0, 0, 0, 0), parts[p]].astype(f32)
@@ -820,15 +831,19 @@
         def cornered():
             hop(k, 0).wait_send()
             hop(k, 2).wait_send()
-        if k == 2:
-            when(end, cornered)
+        if k == 3:
+            cornered()
         elif k != 1:
-            cornered()
+            when(end if k else mid, cornered)
         if k:
             home(k, 0).wait_send()
         if k in (1, 2):
             home(k, 1).wait_send()
-    when(end, lambda: detour().wait_send())
+
+    @pl.when(end)
+    def _():
+        detour().wait_send()
+        ferry(0).wait_send()
     ferry(1).wait_send()
     flow_sent(0)
 
@@ -851,7 +866,7 @@
         pltpu.VMEM((depth * 8, feat, tok), bf16), pltpu.VMEM((depth * 4, feat, tok), bf16),
         pltpu.VMEM((depth * 2, half, tok), bf16), pltpu.VMEM((depth * 2, rest, tok), bf16),
         pltpu.VMEM((depth, half, tok), bf16), pltpu.VMEM((depth, rest, tok), bf16),
-        pltpu.VMEM((depth - 1, feat, tok), bf16), pltpu.VMEM((2, feat, tok), bf16),
+        pltpu.VMEM((depth - 1, feat, tok), bf16), pltpu.VMEM((3, feat, tok), bf16),
         pltpu.VMEM((rest, tok), bf16),
         pltpu.VMEM((2, experts, ff, width), bf16), pltpu.VMEM((experts, width, ff), bf16),
         pltpu.VMEM((ff, width), bf16),
@@ -865,7 +880,7 @@
         dma((5, 2)), dma((depth, 2)), dma((depth, 6)), dma((depth, 6)),
         dma((depth, 8)), dma((depth, 8)), dma((depth, 4)), dma((depth, 4)),
         dma((depth, 6)), dma((depth, 6)), dma((depth, 2)), dma((depth, 2)),
-        dma((3, 2)), dma((2, 2)), dma((2,)), dma((2,)), dma((2,)),
+        dma((3, 2)), dma((2, 2)), dma((3,)), dma((3,)), dma((2,)),
     ]
     mixed = pl.pallas_call(
         fused_kernel,

time: 104 us -> 101 us (0.971)
  Pallas kernels: 102 us -> 99.4 us
    pallas_call x1, Pallas kernels: 102 us -> 99.4 us  [fused(): pl.pallas_call(fused_kernel, out_shape=jax.ShapeDtypeStruct((feat, tok),...]
where the time goes in v5:
time: 101 us
  Pallas kernels  99.4 us (98%)
  local copies, waits for them, and re-layouts  1.75 us (2%)
    pallas_call x1, Pallas kernels, fused(): pl.pallas_call(fused_kernel, out_shape=jax.ShapeDtypeStruct((feat, tok),...  99.4 us

profile of v5, /device:TPU:0, one launch (start us, length us, event | category | flops | bytes accessed | tf_op | source)
XLA Modules:
  0.0 101.2 jit_solution(7341821788362172298)
XLA Ops:
  0.0 99.4 %shard_map.64 = bf16[720,256]{1,0:T(8,128)(2,1)} custom-call(bf16[720,256]{1,0:T(8,128)(2,1)} %bitcast.9, s32[4,256]{1,0:T(4,128)} %bitcast.10, f32[4,256]{1,0:T(4,128)} %bitcast.11, bf16[2,720,2880]{2,1,0:T(8,128)(2,1)} %bitcast.6, bf16[2,720,2880]{2,1,0:T(8,128)(2,1)} %bitcast.7, bf16[2,720,2880]{2,1,0:T(8,128)(2,1)} %down.1), custom_call_target="tpu_custom_call" | custom-call | tf_op jit(solution)/shard_map/pallas_call | solution.py:885
  99.4 1.7 %copy.8 = bf16[256,720]{0,1:T(8,128)(2,1)} copy(bf16[256,720]{0,1:T(8,128)(2,1)} %bitcast.8) | data formatting | bytes 737280

commit v6 on v5

--- a/solution.py
+++ b/solution.py
@@ -719,14 +719,18 @@
 
         @at((k == 0) & mid)
         def _():
-            scatter_far(3)
+            scatter_corner(3)
+
+        @at(k == last)
+        def _():
+            when(mid, lambda: scatter_ferry(2))
+            when(end, lambda: scatter_corner(2))
+        enter(k, 0)
+
+        @at((k == 0) & mid)
+        def _():
+            scatter_sides(3)
             scatter_end(2)
-
-        @at(k == last)
-        def _():
-            when(mid, lambda: scatter_ferry(2))
-            when(end, lambda: scatter_far(2))
-        enter(k, 0)
 
         @at((k == 0) & end)
         def _():
@@ -745,6 +749,7 @@
         @at(k == last)
         def _():
             when(mid, lambda: scatter_near(2))
+            when(end, lambda: scatter_sides(2))
             scatter_end(1)
         leave(0)
 

time: 101 us -> 101 us (level)
  no operation moved by 1% of the time
where the time goes in v6:
time: 101 us
  Pallas kernels  99.3 us (98%)
  local copies, waits for them, and re-layouts  1.75 us (2%)
    pallas_call x1, Pallas kernels, fused(): pl.pallas_call(fused_kernel, out_shape=jax.ShapeDtypeStruct((feat, tok),...  99.3 us

profile of v6, /device:TPU:0, one launch (start us, length us, event | category | flops | bytes accessed | tf_op | source)
XLA Modules:
  0.0 101.1 jit_solution(5848535813753060555)
XLA Ops:
  0.0 99.3 %shard_map.64 = bf16[720,256]{1,0:T(8,128)(2,1)} custom-call(bf16[720,256]{1,0:T(8,128)(2,1)} %bitcast.9, s32[4,256]{1,0:T(4,128)} %bitcast.10, f32[4,256]{1,0:T(4,128)} %bitcast.11, bf16[2,720,2880]{2,1,0:T(8,128)(2,1)} %bitcast.6, bf16[2,720,2880]{2,1,0:T(8,128)(2,1)} %bitcast.7, bf16[2,720,2880]{2,1,0:T(8,128)(2,1)} %down.1), custom_call_target="tpu_custom_call" | custom-call | tf_op jit(solution)/shard_map/pallas_call | solution.py:890
  99.3 1.7 %copy.8 = bf16[256,720]{0,1:T(8,128)(2,1)} copy(bf16[256,720]{0,1:T(8,128)(2,1)} %bitcast.8) | data formatting | bytes 737280
